TPU v7x, 256 devices: a whole 4x4x8 slice. The times are simulated.
256 devices in a mesh: lat: 8 (over z), lon: 16 (over x, y), obs: 2 (over core).
Axes of the slice: x: 4, y: 4, z: 8, core: 2. Of those that a mesh axis runs over, the one named last changes fastest.
Arguments:
- innovation: float32 [32768, 128], P(('lat', 'lon', 'obs')), may hold values from -6 to 6
- obs_error: float32 [32768, 128], P(('lat', 'lon', 'obs')), may hold values from 0.5 to 2
- obs_offset: float32 [2, 32768, 128], P(None, ('lat', 'lon', 'obs')), may hold values from 0 to 1
- obs_cell: int32 [32768, 128], P(('lat', 'lon', 'obs')), may hold values from 0 to 65535
- obs_owner: int32 [256, 128], P(('lat', 'lon', 'obs')), may hold values from 0 to 127, as said below
- block_count: int32 [256], P(('lat', 'lon', 'obs')), may hold values from 64 to 128
- land_mask: int32 [512, 16384], P(('lat', 'obs'), 'lon'), may hold values from 0 to 1, as said below
- inertia: float32 [512, 16384], P(('lat', 'obs'), 'lon'), may hold values from 0.002 to 0.05
- sea_depth: float32 [512, 16384], P(('lat', 'obs'), 'lon'), may hold values from 0.5 to 5
Outputs:
- adjoint_field: float32 [512, 16384], P(('lat', 'obs'), 'lon')
- residual: float32 [512, 16384], P(('lat', 'obs'), 'lon')
Inputs may be any that keep to these rules, and one draw needn't show every extreme that they name: `obs_owner`: among the live blocks of one device at most 3 name the same tile; in every draw some tile is named by exactly 3 live blocks of every device. `land_mask`: the first and the last grid row are land.
All inputs are finite; a program needn't handle non-finite values.
Results may differ from a plain program's by a relative error of at most 0.0003.
Values sent between devices are 32-bit elements; how exact they have to be, the bound alone decides.
A program may use at most 64 MiB of HBM per device.

v0:
```python
import jax
import jax.numpy as jnp
from jax import lax
from jax.sharding import Mesh
from jax.sharding import PartitionSpec as P

ITERS = 5
LON = ("lon_0", "lon_1")
LAT_LON_OBS = ("lat", "lon_0", "lon_1", "obs")
LAT_LON = ("lat", "lon_0", "lon_1")


def extended(block, sides, width):
    for axis, dim in sides:
        count = lax.axis_size(axis)
        forward = [(i, i + 1) for i in range(count - 1)]
        forward.append((count - 1, 0))
        backward = [(target, source) for source, target in forward]
        low = lax.ppermute(
            lax.slice_in_dim(block, block.shape[dim] - width, None, axis=dim), axis, forward
        )
        high = lax.ppermute(lax.slice_in_dim(block, 0, width, axis=dim), axis, backward)
        block = jnp.concatenate([low, block, high], axis=dim)
    return block


def by_axis(value, axes):
    for axis in axes:
        value = lax.psum(value, axis)
    return value


def cut_along(value, dim, peers):
    shape = value.shape
    tiles = value.reshape(*shape[:dim], peers, shape[dim] // peers, *shape[dim + 1 :])
    return jnp.moveaxis(tiles, dim, 0)


def in_order(tiles, dim):
    tiles = jnp.moveaxis(tiles, 0, dim)
    shape = tiles.shape
    return tiles.reshape(*shape[:dim], shape[dim] * shape[dim + 1], *shape[dim + 2 :])


def exchange_both(value, axis, axes, splits, concats):
    sizes = [lax.axis_size(a) for a in axes]
    tiles = cut_along(value, splits[0], sizes[0])
    tiles = jnp.moveaxis(cut_along(tiles, splits[1] + 1, sizes[1]), 0, 1)
    inside = tiles.shape[2:]
    tiles = tiles.reshape(-1, *inside)
    tiles = lax.all_to_all(tiles, axis, split_axis=0, concat_axis=0, tiled=True)
    tiles = in_order(tiles.reshape(*sizes, *inside), concats[0] + 1)
    return in_order(tiles, concats[1])


def shifted(value, axis, steps):
    count = lax.axis_size(axis)
    pairs = [(source, (source + steps) % count) for source in range(count)]
    return lax.ppermute(value, axis, pairs)


def shifted_2(block, axis, distance):
    devices = range(lax.axis_size(axis))
    route = [(i - distance, i) for i in devices if i - distance in devices]
    return lax.ppermute(block, axis, route)


def sent_and_summed(value, axis, dim):
    tiles = cut_along(value, dim, lax.axis_size(axis))
    arrived = lax.all_to_all(tiles, axis, split_axis=0, concat_axis=0, tiled=True)
    return arrived.sum(axis=0)


def border(field):
    return extended(field, ((("lat", "obs"), 0), (LON, 1)), 1)


def two_products(residual, applied):
    return (
        by_axis(jnp.sum(residual * residual), LAT_LON_OBS),
        by_axis(jnp.sum(residual * applied), LAT_LON_OBS),
    )


def body(
    innovation,
    obs_error,
    obs_offset,
    obs_cell,
    obs_owner,
    block_count,
    land_mask,
    inertia,
    sea_depth,
):
    block_total = obs_owner.shape[1]
    block_width = innovation.shape[1]
    n_lat = lax.axis_size("lat")
    n_lon = lax.axis_size(LON)
    tile_count = n_lat * n_lon
    capacity = max(3, 2 * ((block_total + tile_count - 1) // tile_count))
    slot_total = tile_count * capacity
    tile_rows = land_mask.shape[0] * lax.axis_size("obs")
    tile_cols = land_mask.shape[1]
    owners = obs_owner[0]
    block_ids = jnp.arange(block_total)
    is_live = block_ids < block_count[0]
    earlier = block_ids[None, :] < block_ids[:, None]
    same_owner = (owners[None, :] == owners[:, None]) & earlier & is_live[None, :]
    slot_rank = jnp.sum(same_owner.astype(jnp.int32), axis=1)
    target = jnp.where(is_live, owners * capacity + slot_rank, slot_total)
    scaled = innovation / (obs_error * obs_error)
    floats = jnp.stack([scaled, obs_offset[0], obs_offset[1]], axis=1)

    def put_slots(values):
        holder = jnp.zeros((slot_total + 1,) + values.shape[1:], values.dtype)
        return holder.at[target].set(values)[:slot_total]

    sent_floats = put_slots(floats)
    sent_cells = put_slots(obs_cell)
    received, cell_ids = (
        exchange_both(
            sent_floats.reshape(n_lat, n_lon, capacity, 3, block_width),
            LAT_LON,
            ("lat", LON),
            (0, 1),
            (0, 1),
        ),
        exchange_both(
            sent_cells.reshape(n_lat, n_lon, capacity, block_width),
            LAT_LON,
            ("lat", LON),
            (0, 1),
            (0, 1),
        ),
    )
    received = received.reshape(-1, 3, block_width)
    cell_ids = cell_ids.reshape(-1, block_width)
    group = 1
    for size_try in range(1, slot_total + 1):
        if slot_total % size_try == 0 and size_try * block_width <= 4096:
            group = size_try
    turns = slot_total // group
    group_obs = group * block_width
    scaled_in = received[:, 0].reshape(turns, group_obs)
    north_frac = received[:, 1].reshape(turns, group_obs)
    east_frac = received[:, 2].reshape(turns, group_obs)
    cells_in = cell_ids.reshape(turns, group_obs)
    wide = tile_cols + 1
    row_axis = jnp.arange(tile_rows + 1, dtype=jnp.int32)[:, None]
    col_axis = jnp.arange(wide, dtype=jnp.int32)[None, :]

    def spread(total, pieces):
        amount, north, east, cells = pieces
        cell_row = (cells // tile_cols)[None, :]
        cell_col = (cells % tile_cols)[:, None]
        row_weights = (
            jnp.where(row_axis == cell_row, 1.0 - north[None, :], 0.0)
            + jnp.where(row_axis == cell_row + 1, north[None, :], 0.0)
        ) * amount[None, :]
        col_weights = jnp.where(col_axis == cell_col, 1.0 - east[:, None], 0.0) + jnp.where(
            col_axis == cell_col + 1, east[:, None], 0.0
        )
        return (
            total
            + jnp.dot(
                row_weights,
                col_weights,
                precision=lax.Precision.HIGHEST,
                preferred_element_type=jnp.float32,
            ),
            None,
        )

    partial_value, unused = lax.scan(
        spread,
        jnp.zeros((tile_rows + 1, wide), jnp.float32),
        (scaled_in, north_frac, east_frac, cells_in),
    )
    arrived_col = shifted(partial_value[:, tile_cols], LON, 1)
    partial_value = partial_value[:, :tile_cols].at[:, 0].add(arrived_col)
    arrived_row = shifted_2(partial_value[tile_rows], "lat", 1)
    tile_part = partial_value[:tile_rows].at[0].add(arrived_row)
    ocean = land_mask.astype(jnp.float32)
    forcing = sent_and_summed(tile_part, "obs", 0) * ocean
    conduct = ocean * sea_depth
    padded = border(conduct)
    cond_north = jnp.sqrt(conduct * padded[:-2, 1:-1])
    cond_south = jnp.sqrt(conduct * padded[2:, 1:-1])
    cond_west = jnp.sqrt(conduct * padded[1:-1, :-2])
    cond_east = jnp.sqrt(conduct * padded[1:-1, 2:])
    diagonal = inertia + cond_north + cond_south + cond_west + cond_east

    def operate(field):
        outer = border(field)
        return (
            diagonal * field
            - cond_north * outer[:-2, 1:-1]
            - cond_south * outer[2:, 1:-1]
            - cond_west * outer[1:-1, :-2]
            - cond_east * outer[1:-1, 2:]
        )

    adjoint_field = jnp.zeros_like(forcing)
    residual = forcing
    applied = operate(residual)
    norm_now, product = two_products(residual, applied)
    step_size = norm_now / product
    direction = residual
    applied_dir = applied
    for iteration in range(ITERS):
        adjoint_field = adjoint_field + step_size * direction
        residual = residual - step_size * applied_dir
        if iteration + 1 < ITERS:
            applied = operate(residual)
            norm_next, product = two_products(residual, applied)
            beta_ratio = norm_next / norm_now
            step_size = norm_next / (product - beta_ratio * norm_next / step_size)
            direction = residual + beta_ratio * direction
            applied_dir = applied + beta_ratio * applied_dir
            norm_now = norm_next
    return (adjoint_field, residual)


def solution(mesh):
    split = Mesh(
        mesh.devices.reshape(mesh.shape["lat"], 4, 4, mesh.shape["obs"]),
        ("lat", "lon_0", "lon_1", "obs"),
    )
    return jax.shard_map(
        body,
        mesh=split,
        in_specs=(
            P(LAT_LON_OBS, None),
            P(LAT_LON_OBS, None),
            P(None, LAT_LON_OBS, None),
            P(LAT_LON_OBS, None),
            P(LAT_LON_OBS, None),
            P(LAT_LON_OBS),
            P(("lat", "obs"), LON),
            P(("lat", "obs"), LON),
            P(("lat", "obs"), LON),
        ),
        out_specs=(P(("lat", "obs"), LON), P(("lat", "obs"), LON)),
        check_vma=False,
    )
```

profile of v0, /device:TPU:1, one launch (start us, length us, event | category | flops | bytes accessed | tf_op | source)
XLA Modules:
  0.0 612.2 jit_solution(17351134791260999394)
XLA Ops:
  4.8 16.3 %all-to-all-start = ((s32[128,1,1,3,128]{4,2,3,1,0:T(1,128)}), s32[128,1,1,3,128]{4,2,3,1,0:T(1,128)S(1)}, u32[]{:S(2)}, u32[]{:S(2)}) async-start(s32[128,1,1,3,128]{4,2,3,1,0:T(1,128)} %bitcast.5), calls=%async_computation | async-start | bytes 393216 | tf_op jit(solution)/shard_map/all_to_all | solution.py:51
  21.5 4.5 scatter_fusion
  27.5 5.6 all-to-all-done
  33.1 7.5 %all-to-all-start.1 = ((f32[128,1,1,3,3,128]{5,2,4,3,1,0:T(1,128)}), f32[128,1,1,3,3,128]{5,2,4,3,1,0:T(1,128)S(1)}, u32[]{:S(2)}, u32[]{:S(2)}) async-start(f32[128,1,1,3,3,128]{5,2,4,3,1,0:T(1,128)} %copy.29), calls=%async_computation.1 | async-start | bytes 1179648 | tf_op jit(solution)/shard_map/all_to_all | solution.py:51
  40.8 19.1 %all-to-all-done.1 = f32[128,1,1,3,3,128]{5,2,4,3,1,0:T(1,128)S(1)} async-done(((f32[128,1,1,3,3,128]{5,2,4,3,1,0:T(1,128)}), f32[128,1,1,3,3,128]{5,2,4,3,1,0:T(1,128)S(1)}, u32[]{:S(2)}, u32[]{:S(2)}) %all-to-all-start.1) | async-done | bytes 589856 | tf_op jit(solution)/shard_map/all_to_all | solution.py:51
  60.6 239.6 %while.16 = (s32[]{:T(128)}, f32[65,1025]{1,0:T(8,128)S(1)}, s32[12,4096]{1,0:T(8,128)S(1)}, f32[12,4096]{1,0:T(8,128)S(1)}, f32[12,4096]{1,0:T(8,128)S(1)}, /*index=5*/f32[12,4096]{1,0:T(8,128)S(1)}, s32[]{:T(128)}, s32[]{:T(128)}) while((s32[]{:T(128)}, f32[65,1025]{1,0:T(8,128)S(1)}, s32[12,4096]{1,0:T(8,128)S(1)}, ...), condition=%wide.region_4.5_spmd.clone.clone, body=%wide.region_3.4_spmd.clone.clone.sunk | while | flops 3297597440 | bytes 942707 | solution.py:175
  72.4 18.7 %fusion.98 = f32[65,1025]{1,0:T(8,128)S(1)} fusion(f32[4096]{0:T(1024)S(1)} %bitcast.80, s32[4096]{0:T(1024)S(1)} %get-tuple-element.342, f32[4096]{0:T(1024)S(1)} %broadcast_subtract_fusion.5, s32[4096]{0:T(1024)S(1)} %get-tuple-element.343, f32[4096]{0:T(1024)S(1)} %bitcast.87, f32[4096]{0:T(1024)S(1)} %bitcast.86, s32[4096]{0:T(1024)S(1)} %bitcast.88, ...), kind=kOutput, calls=%fused_computation.15.clone.1 | convolution fusion | flops 3297474560 | bytes 680457 | tf_op jit(solution)/shard_map/while/body/eval_jaxpr/dot_general | solution.py:166
  91.4 18.7 %fusion.98 = f32[65,1025]{1,0:T(8,128)S(1)} fusion(f32[4096]{0:T(1024)S(1)} %bitcast.80, s32[4096]{0:T(1024)S(1)} %get-tuple-element.342, f32[4096]{0:T(1024)S(1)} %broadcast_subtract_fusion.5, s32[4096]{0:T(1024)S(1)} %get-tuple-element.343, f32[4096]{0:T(1024)S(1)} %bitcast.87, f32[4096]{0:T(1024)S(1)} %bitcast.86, s32[4096]{0:T(1024)S(1)} %bitcast.88, ...), kind=kOutput, calls=%fused_computation.15.clone.1 | convolution fusion | flops 3297474560 | bytes 680457 | tf_op jit(solution)/shard_map/while/body/eval_jaxpr/dot_general | solution.py:166
  110.4 18.7 %fusion.98 = f32[65,1025]{1,0:T(8,128)S(1)} fusion(f32[4096]{0:T(1024)S(1)} %bitcast.80, s32[4096]{0:T(1024)S(1)} %get-tuple-element.342, f32[4096]{0:T(1024)S(1)} %broadcast_subtract_fusion.5, s32[4096]{0:T(1024)S(1)} %get-tuple-element.343, f32[4096]{0:T(1024)S(1)} %bitcast.87, f32[4096]{0:T(1024)S(1)} %bitcast.86, s32[4096]{0:T(1024)S(1)} %bitcast.88, ...), kind=kOutput, calls=%fused_computation.15.clone.1 | convolution fusion | flops 3297474560 | bytes 680457 | tf_op jit(solution)/shard_map/while/body/eval_jaxpr/dot_general | solution.py:166
  129.4 18.7 %fusion.98 = f32[65,1025]{1,0:T(8,128)S(1)} fusion(f32[4096]{0:T(1024)S(1)} %bitcast.80, s32[4096]{0:T(1024)S(1)} %get-tuple-element.342, f32[4096]{0:T(1024)S(1)} %broadcast_subtract_fusion.5, s32[4096]{0:T(1024)S(1)} %get-tuple-element.343, f32[4096]{0:T(1024)S(1)} %bitcast.87, f32[4096]{0:T(1024)S(1)} %bitcast.86, s32[4096]{0:T(1024)S(1)} %bitcast.88, ...), kind=kOutput, calls=%fused_computation.15.clone.1 | convolution fusion | flops 3297474560 | bytes 680457 | tf_op jit(solution)/shard_map/while/body/eval_jaxpr/dot_general | solution.py:166
  148.4 18.7 %fusion.98 = f32[65,1025]{1,0:T(8,128)S(1)} fusion(f32[4096]{0:T(1024)S(1)} %bitcast.80, s32[4096]{0:T(1024)S(1)} %get-tuple-element.342, f32[4096]{0:T(1024)S(1)} %broadcast_subtract_fusion.5, s32[4096]{0:T(1024)S(1)} %get-tuple-element.343, f32[4096]{0:T(1024)S(1)} %bitcast.87, f32[4096]{0:T(1024)S(1)} %bitcast.86, s32[4096]{0:T(1024)S(1)} %bitcast.88, ...), kind=kOutput, calls=%fused_computation.15.clone.1 | convolution fusion | flops 3297474560 | bytes 680457 | tf_op jit(solution)/shard_map/while/body/eval_jaxpr/dot_general | solution.py:166
  167.4 18.7 %fusion.98 = f32[65,1025]{1,0:T(8,128)S(1)} fusion(f32[4096]{0:T(1024)S(1)} %bitcast.80, s32[4096]{0:T(1024)S(1)} %get-tuple-element.342, f32[4096]{0:T(1024)S(1)} %broadcast_subtract_fusion.5, s32[4096]{0:T(1024)S(1)} %get-tuple-element.343, f32[4096]{0:T(1024)S(1)} %bitcast.87, f32[4096]{0:T(1024)S(1)} %bitcast.86, s32[4096]{0:T(1024)S(1)} %bitcast.88, ...), kind=kOutput, calls=%fused_computation.15.clone.1 | convolution fusion | flops 3297474560 | bytes 680457 | tf_op jit(solution)/shard_map/while/body/eval_jaxpr/dot_general | solution.py:166
  186.4 18.7 %fusion.98 = f32[65,1025]{1,0:T(8,128)S(1)} fusion(f32[4096]{0:T(1024)S(1)} %bitcast.80, s32[4096]{0:T(1024)S(1)} %get-tuple-element.342, f32[4096]{0:T(1024)S(1)} %broadcast_subtract_fusion.5, s32[4096]{0:T(1024)S(1)} %get-tuple-element.343, f32[4096]{0:T(1024)S(1)} %bitcast.87, f32[4096]{0:T(1024)S(1)} %bitcast.86, s32[4096]{0:T(1024)S(1)} %bitcast.88, ...), kind=kOutput, calls=%fused_computation.15.clone.1 | convolution fusion | flops 3297474560 | bytes 680457 | tf_op jit(solution)/shard_map/while/body/eval_jaxpr/dot_general | solution.py:166
  205.3 18.7 %fusion.98 = f32[65,1025]{1,0:T(8,128)S(1)} fusion(f32[4096]{0:T(1024)S(1)} %bitcast.80, s32[4096]{0:T(1024)S(1)} %get-tuple-element.342, f32[4096]{0:T(1024)S(1)} %broadcast_subtract_fusion.5, s32[4096]{0:T(1024)S(1)} %get-tuple-element.343, f32[4096]{0:T(1024)S(1)} %bitcast.87, f32[4096]{0:T(1024)S(1)} %bitcast.86, s32[4096]{0:T(1024)S(1)} %bitcast.88, ...), kind=kOutput, calls=%fused_computation.15.clone.1 | convolution fusion | flops 3297474560 | bytes 680457 | tf_op jit(solution)/shard_map/while/body/eval_jaxpr/dot_general | solution.py:166
  224.3 18.7 %fusion.98 = f32[65,1025]{1,0:T(8,128)S(1)} fusion(f32[4096]{0:T(1024)S(1)} %bitcast.80, s32[4096]{0:T(1024)S(1)} %get-tuple-element.342, f32[4096]{0:T(1024)S(1)} %broadcast_subtract_fusion.5, s32[4096]{0:T(1024)S(1)} %get-tuple-element.343, f32[4096]{0:T(1024)S(1)} %bitcast.87, f32[4096]{0:T(1024)S(1)} %bitcast.86, s32[4096]{0:T(1024)S(1)} %bitcast.88, ...), kind=kOutput, calls=%fused_computation.15.clone.1 | convolution fusion | flops 3297474560 | bytes 680457 | tf_op jit(solution)/shard_map/while/body/eval_jaxpr/dot_general | solution.py:166
  243.3 18.7 %fusion.98 = f32[65,1025]{1,0:T(8,128)S(1)} fusion(f32[4096]{0:T(1024)S(1)} %bitcast.80, s32[4096]{0:T(1024)S(1)} %get-tuple-element.342, f32[4096]{0:T(1024)S(1)} %broadcast_subtract_fusion.5, s32[4096]{0:T(1024)S(1)} %get-tuple-element.343, f32[4096]{0:T(1024)S(1)} %bitcast.87, f32[4096]{0:T(1024)S(1)} %bitcast.86, s32[4096]{0:T(1024)S(1)} %bitcast.88, ...), kind=kOutput, calls=%fused_computation.15.clone.1 | convolution fusion | flops 3297474560 | bytes 680457 | tf_op jit(solution)/shard_map/while/body/eval_jaxpr/dot_general | solution.py:166
  262.3 18.7 %fusion.98 = f32[65,1025]{1,0:T(8,128)S(1)} fusion(f32[4096]{0:T(1024)S(1)} %bitcast.80, s32[4096]{0:T(1024)S(1)} %get-tuple-element.342, f32[4096]{0:T(1024)S(1)} %broadcast_subtract_fusion.5, s32[4096]{0:T(1024)S(1)} %get-tuple-element.343, f32[4096]{0:T(1024)S(1)} %bitcast.87, f32[4096]{0:T(1024)S(1)} %bitcast.86, s32[4096]{0:T(1024)S(1)} %bitcast.88, ...), kind=kOutput, calls=%fused_computation.15.clone.1 | convolution fusion | flops 3297474560 | bytes 680457 | tf_op jit(solution)/shard_map/while/body/eval_jaxpr/dot_general | solution.py:166
  281.3 18.7 %fusion.98 = f32[65,1025]{1,0:T(8,128)S(1)} fusion(f32[4096]{0:T(1024)S(1)} %bitcast.80, s32[4096]{0:T(1024)S(1)} %get-tuple-element.342, f32[4096]{0:T(1024)S(1)} %broadcast_subtract_fusion.5, s32[4096]{0:T(1024)S(1)} %get-tuple-element.343, f32[4096]{0:T(1024)S(1)} %bitcast.87, f32[4096]{0:T(1024)S(1)} %bitcast.86, s32[4096]{0:T(1024)S(1)} %bitcast.88, ...), kind=kOutput, calls=%fused_computation.15.clone.1 | convolution fusion | flops 3297474560 | bytes 680457 | tf_op jit(solution)/shard_map/while/body/eval_jaxpr/dot_general | solution.py:166
  301.5 4.7 collective-permute-done
  307.1 2.6 collective-permute-start.1
  310.6 9.1 %all_to_all.15 = f32[2,32,1024]{2,1,0:T(8,128)S(1)} all-to-all(f32[2,32,1024]{2,1,0:T(8,128)S(1)} %bitcast.83), channel_id=1, replica_groups=mesh['lat'=8,'lon_0'=4,'lon_1'=4,'obs'=2] {'obs'}, dimensions={0} | all-to-all | bytes 524288 | tf_op jit(solution)/shard_map/all_to_all | solution.py:70
  325.2 4.8 collective-permute-start.5
  330.1 4.8 collective-permute-start.9
  337.0 13.2 %all-reduce.4 = (f32[]{:T(128)}, f32[]{:T(128)}) all-reduce(f32[]{:T(128)} %get-tuple-element.194, f32[]{:T(128)} %get-tuple-element.193), channel_id=1, replica_groups=mesh['lat'=8,'lon_0'=4,'lon_1'=4,'obs'=2] {'lat'}, use_global_device_ids=true, to_apply=%region_8.9 | all-reduce | flops 2 | bytes 16 | tf_op jit(solution)/shard_map/psum | solution.py:29
  350.1 6.6 %all-reduce.14 = (f32[]{:T(128)}, f32[]{:T(128)}) all-reduce(f32[]{:T(128)} %get-tuple-element.215, f32[]{:T(128)} %get-tuple-element.216), channel_id=1, replica_groups=mesh['lat'=8,'lon_0'=4,'lon_1'=4,'obs'=2] {'lon_0'}, use_global_device_ids=true, to_apply=%region_9.10 | all-reduce | flops 2 | bytes 16 | tf_op jit(solution)/shard_map/psum | solution.py:29
  356.7 11.7 %all-reduce.9 = (f32[]{:T(128)}, f32[]{:T(128)}) all-reduce(f32[]{:T(128)} %get-tuple-element.235, f32[]{:T(128)} %get-tuple-element.236), channel_id=1, replica_groups=mesh['lat'=8,'lon_0'=4,'lon_1'=4,'obs'=2] {'lon_1'}, use_global_device_ids=true, to_apply=%region_10.11 | all-reduce | flops 2 | bytes 16 | tf_op jit(solution)/shard_map/psum | solution.py:29
  368.4 11.4 %all-reduce.19 = (f32[]{:T(128)}, f32[]{:T(128)}) all-reduce(f32[]{:T(128)} %get-tuple-element.225, f32[]{:T(128)} %get-tuple-element.226), channel_id=1, replica_groups=mesh['lat'=8,'lon_0'=4,'lon_1'=4,'obs'=2] {'obs'}, use_global_device_ids=true, to_apply=%region_11.12 | all-reduce | flops 2 | bytes 16 | tf_op jit(solution)/shard_map/psum | solution.py:29
  383.9 2.3 collective-permute-done.11
  386.3 4.8 collective-permute-start.13
  393.6 13.4 %all-reduce.3 = (f32[]{:T(128)}, f32[]{:T(128)}) all-reduce(f32[]{:T(128)} %get-tuple-element.192, f32[]{:T(128)} %get-tuple-element.191), channel_id=1, replica_groups=mesh['lat'=8,'lon_0'=4,'lon_1'=4,'obs'=2] {'lat'}, use_global_device_ids=true, to_apply=%region_18.19 | all-reduce | flops 2 | bytes 16 | tf_op jit(solution)/shard_map/psum | solution.py:29
  407.0 6.7 %all-reduce.13 = (f32[]{:T(128)}, f32[]{:T(128)}) all-reduce(f32[]{:T(128)} %get-tuple-element.213, f32[]{:T(128)} %get-tuple-element.214), channel_id=1, replica_groups=mesh['lat'=8,'lon_0'=4,'lon_1'=4,'obs'=2] {'lon_0'}, use_global_device_ids=true, to_apply=%region_19.20 | all-reduce | flops 2 | bytes 16 | tf_op jit(solution)/shard_map/psum | solution.py:29
  413.6 11.9 %all-reduce.8 = (f32[]{:T(128)}, f32[]{:T(128)}) all-reduce(f32[]{:T(128)} %get-tuple-element.233, f32[]{:T(128)} %get-tuple-element.234), channel_id=1, replica_groups=mesh['lat'=8,'lon_0'=4,'lon_1'=4,'obs'=2] {'lon_1'}, use_global_device_ids=true, to_apply=%region_20.21 | all-reduce | flops 2 | bytes 16 | tf_op jit(solution)/shard_map/psum | solution.py:29
  425.5 9.6 %all-reduce.18 = (f32[]{:T(128)}, f32[]{:T(128)}) all-reduce(f32[]{:T(128)} %get-tuple-element.223, f32[]{:T(128)} %get-tuple-element.224), channel_id=1, replica_groups=mesh['lat'=8,'lon_0'=4,'lon_1'=4,'obs'=2] {'obs'}, use_global_device_ids=true, to_apply=%region_21.22 | all-reduce | flops 2 | bytes 16 | tf_op jit(solution)/shard_map/psum | solution.py:29
  444.1 4.8 collective-permute-start.17
  451.0 14.4 %all-reduce.2 = (f32[]{:T(128)}, f32[]{:T(128)}) all-reduce(f32[]{:T(128)} %get-tuple-element.190, f32[]{:T(128)} %get-tuple-element.189), channel_id=1, replica_groups=mesh['lat'=8,'lon_0'=4,'lon_1'=4,'obs'=2] {'lat'}, use_global_device_ids=true, to_apply=%region_28.29 | all-reduce | flops 2 | bytes 16 | tf_op jit(solution)/shard_map/psum | solution.py:29
  465.3 6.6 %all-reduce.12 = (f32[]{:T(128)}, f32[]{:T(128)}) all-reduce(f32[]{:T(128)} %get-tuple-element.211, f32[]{:T(128)} %get-tuple-element.212), channel_id=1, replica_groups=mesh['lat'=8,'lon_0'=4,'lon_1'=4,'obs'=2] {'lon_0'}, use_global_device_ids=true, to_apply=%region_29.30 | all-reduce | flops 2 | bytes 16 | tf_op jit(solution)/shard_map/psum | solution.py:29
  471.9 11.9 %all-reduce.7 = (f32[]{:T(128)}, f32[]{:T(128)}) all-reduce(f32[]{:T(128)} %get-tuple-element.231, f32[]{:T(128)} %get-tuple-element.232), channel_id=1, replica_groups=mesh['lat'=8,'lon_0'=4,'lon_1'=4,'obs'=2] {'lon_1'}, use_global_device_ids=true, to_apply=%region_30.31 | all-reduce | flops 2 | bytes 16 | tf_op jit(solution)/shard_map/psum | solution.py:29
  483.9 8.8 %all-reduce.17 = (f32[]{:T(128)}, f32[]{:T(128)}) all-reduce(f32[]{:T(128)} %get-tuple-element.221, f32[]{:T(128)} %get-tuple-element.222), channel_id=1, replica_groups=mesh['lat'=8,'lon_0'=4,'lon_1'=4,'obs'=2] {'obs'}, use_global_device_ids=true, to_apply=%region_31.32 | all-reduce | flops 2 | bytes 16 | tf_op jit(solution)/shard_map/psum | solution.py:29
  501.8 4.8 collective-permute-start.21
  509.0 13.4 %all-reduce.1 = (f32[]{:T(128)}, f32[]{:T(128)}) all-reduce(f32[]{:T(128)} %get-tuple-element.188, f32[]{:T(128)} %get-tuple-element.187), channel_id=1, replica_groups=mesh['lat'=8,'lon_0'=4,'lon_1'=4,'obs'=2] {'lat'}, use_global_device_ids=true, to_apply=%region_38.39 | all-reduce | flops 2 | bytes 16 | tf_op jit(solution)/shard_map/psum | solution.py:29
  522.4 6.6 %all-reduce.11 = (f32[]{:T(128)}, f32[]{:T(128)}) all-reduce(f32[]{:T(128)} %get-tuple-element.209, f32[]{:T(128)} %get-tuple-element.210), channel_id=1, replica_groups=mesh['lat'=8,'lon_0'=4,'lon_1'=4,'obs'=2] {'lon_0'}, use_global_device_ids=true, to_apply=%region_39.40 | all-reduce | flops 2 | bytes 16 | tf_op jit(solution)/shard_map/psum | solution.py:29
  529.0 11.9 %all-reduce.6 = (f32[]{:T(128)}, f32[]{:T(128)}) all-reduce(f32[]{:T(128)} %get-tuple-element.229, f32[]{:T(128)} %get-tuple-element.230), channel_id=1, replica_groups=mesh['lat'=8,'lon_0'=4,'lon_1'=4,'obs'=2] {'lon_1'}, use_global_device_ids=true, to_apply=%region_40.41 | all-reduce | flops 2 | bytes 16 | tf_op jit(solution)/shard_map/psum | solution.py:29
  540.9 9.5 %all-reduce.16 = (f32[]{:T(128)}, f32[]{:T(128)}) all-reduce(f32[]{:T(128)} %get-tuple-element.219, f32[]{:T(128)} %get-tuple-element.220), channel_id=1, replica_groups=mesh['lat'=8,'lon_0'=4,'lon_1'=4,'obs'=2] {'obs'}, use_global_device_ids=true, to_apply=%region_41.42 | all-reduce | flops 2 | bytes 16 | tf_op jit(solution)/shard_map/psum | solution.py:29
  558.6 4.8 collective-permute-start.25
  565.4 14.4 %all-reduce = (f32[]{:T(128)}, f32[]{:T(128)}) all-reduce(f32[]{:T(128)} %get-tuple-element.186, f32[]{:T(128)} %get-tuple-element.185), channel_id=1, replica_groups=mesh['lat'=8,'lon_0'=4,'lon_1'=4,'obs'=2] {'lat'}, use_global_device_ids=true, to_apply=%region_48.49 | all-reduce | flops 2 | bytes 16 | tf_op jit(solution)/shard_map/psum | solution.py:29
  579.8 6.6 %all-reduce.10 = (f32[]{:T(128)}, f32[]{:T(128)}) all-reduce(f32[]{:T(128)} %get-tuple-element.207, f32[]{:T(128)} %get-tuple-element.208), channel_id=1, replica_groups=mesh['lat'=8,'lon_0'=4,'lon_1'=4,'obs'=2] {'lon_0'}, use_global_device_ids=true, to_apply=%region_49.50 | all-reduce | flops 2 | bytes 16 | tf_op jit(solution)/shard_map/psum | solution.py:29
  586.4 11.9 %all-reduce.5 = (f32[]{:T(128)}, f32[]{:T(128)}) all-reduce(f32[]{:T(128)} %get-tuple-element.227, f32[]{:T(128)} %get-tuple-element.228), channel_id=1, replica_groups=mesh['lat'=8,'lon_0'=4,'lon_1'=4,'obs'=2] {'lon_1'}, use_global_device_ids=true, to_apply=%region_50.51 | all-reduce | flops 2 | bytes 16 | tf_op jit(solution)/shard_map/psum | solution.py:29
  598.3 8.8 %all-reduce.15 = (f32[]{:T(128)}, f32[]{:T(128)}) all-reduce(f32[]{:T(128)} %get-tuple-element.217, f32[]{:T(128)} %get-tuple-element.218), channel_id=1, replica_groups=mesh['lat'=8,'lon_0'=4,'lon_1'=4,'obs'=2] {'obs'}, use_global_device_ids=true, to_apply=%region_51.52 | all-reduce | flops 2 | bytes 16 | tf_op jit(solution)/shard_map/psum | solution.py:29
  (171 shorter events, 45.6 us)
Async XLA Ops:
  0.6 20.5 %copy-start.3 = (f32[2,128,128]{2,1,0:T(8,128)S(1)}, f32[2,128,128]{2,1,0:T(8,128)}, u32[]{:S(2)}) copy-start(f32[2,128,128]{2,1,0:T(8,128)} %param.17) | copy-start | bytes 393220
  0.6 20.6 %copy-start.4 = (f32[128,128]{1,0:T(8,128)S(1)}, f32[128,128]{1,0:T(8,128)}, u32[]{:S(2)}) copy-start(f32[128,128]{1,0:T(8,128)} %param.15) | copy-start | bytes 196612
  0.7 20.6 %copy-start.5 = (f32[128,128]{1,0:T(8,128)S(1)}, f32[128,128]{1,0:T(8,128)}, u32[]{:S(2)}) copy-start(f32[128,128]{1,0:T(8,128)} %param.16) | copy-start | bytes 196612
  4.8 28.3 %all-to-all-start = ((s32[128,1,1,3,128]{4,2,3,1,0:T(1,128)}), s32[128,1,1,3,128]{4,2,3,1,0:T(1,128)S(1)}, u32[]{:S(2)}, u32[]{:S(2)}) async-start(s32[128,1,1,3,128]{4,2,3,1,0:T(1,128)} %bitcast.5), calls=%async_computation | async-start | bytes 393216 | tf_op jit(solution)/shard_map/all_to_all | solution.py:51
  33.1 26.8 %all-to-all-start.1 = ((f32[128,1,1,3,3,128]{5,2,4,3,1,0:T(1,128)}), f32[128,1,1,3,3,128]{5,2,4,3,1,0:T(1,128)S(1)}, u32[]{:S(2)}, u32[]{:S(2)}) async-start(f32[128,1,1,3,3,128]{5,2,4,3,1,0:T(1,128)} %copy.29), calls=%async_computation.1 | async-start | bytes 1179648 | tf_op jit(solution)/shard_map/all_to_all | solution.py:51
  300.3 5.8 collective-permute-start
  306.8 12.9 %copy-start.1 = (f32[32,1024]{1,0:T(8,128)S(1)}, f32[32,1024]{1,0:T(8,128)}, u32[]{:S(2)}) copy-start(f32[32,1024]{1,0:T(8,128)} %param.23) | copy-start | bytes 393220
  306.8 12.9 %copy-start.2 = (s32[32,1024]{1,0:T(8,128)S(1)}, s32[32,1024]{1,0:T(8,128)}, u32[]{:S(2)}) copy-start(s32[32,1024]{1,0:T(8,128)} %param.21) | copy-start | bytes 393220
  307.1 3.4 collective-permute-start.1
  319.7 16.3 %copy-start = (f32[32,1024]{1,0:T(8,128)S(1)}, f32[32,1024]{1,0:T(8,128)}, u32[]{:S(2)}) copy-start(f32[32,1024]{1,0:T(8,128)} %param.22) | copy-start | bytes 393220
  319.8 4.0 collective-permute-start.2
  322.0 3.0 collective-permute-start.3
  322.1 7.9 %collective-permute-start.6 = (f32[1,1024]{1,0:T(1,128)S(1)}, f32[1,1024]{1,0:T(1,128)S(1)}, u32[]{:S(2)}, u32[]{:S(2)}) collective-permute-start(f32[1,1024]{1,0:T(1,128)S(1)} %get-tuple-element.291), channel_id=1, source_target_pairs={{0,1},{1,32},{32,33},{33,64},{64,65},{65,96},{96,97},{97,128},{128... | collective-permute-start | bytes 12296 | tf_op jit(solution)/shard_map/ppermute | solution.py:19
  323.8 6.2 %collective-permute-start.7 = (f32[1,1024]{1,0:T(1,128)S(1)}, f32[1,1024]{1,0:T(1,128)S(1)}, u32[]{:S(2)}, u32[]{:S(2)}) collective-permute-start(f32[1,1024]{1,0:T(1,128)S(1)} %get-tuple-element.292), channel_id=1, source_target_pairs={{1,0},{32,1},{33,32},{64,33},{65,64},{96,65},{97,96},{128,97},{129... | collective-permute-start | bytes 12296 | tf_op jit(solution)/shard_map/ppermute | solution.py:22
  325.2 9.7 %collective-permute-start.4 = (f32[34,1]{1,0:T(8,128)S(1)}, f32[34,1]{1,0:T(8,128)S(1)}, u32[]{:S(2)}, u32[]{:S(2)}) collective-permute-start(f32[34,1]{1,0:T(8,128)S(1)} %get-tuple-element.273), channel_id=1, source_target_pairs={{0,2},{2,4},{4,6},{6,8},{8,10},{10,12},{12,14},{14,16},{16,18},{18... | collective-permute-start | bytes 416 | tf_op jit(solution)/shard_map/ppermute | solution.py:19
  325.2 9.7 %collective-permute-start.5 = (f32[34,1]{1,0:T(8,128)S(1)}, f32[34,1]{1,0:T(8,128)S(1)}, u32[]{:S(2)}, u32[]{:S(2)}) collective-permute-start(f32[34,1]{1,0:T(8,128)S(1)} %get-tuple-element.274), channel_id=1, source_target_pairs={{2,0},{4,2},{6,4},{8,6},{10,8},{12,10},{14,12},{16,14},{18,16},{20... | collective-permute-start | bytes 416 | tf_op jit(solution)/shard_map/ppermute | solution.py:22
  330.0 6.0 collective-permute-start.8
  330.1 5.9 collective-permute-start.9
  381.2 2.7 collective-permute-start.10
  383.1 3.0 collective-permute-start.11
  386.2 6.4 %collective-permute-start.12 = (f32[34,1]{1,0:T(8,128)S(1)}, f32[34,1]{1,0:T(8,128)S(1)}, u32[]{:S(2)}, u32[]{:S(2)}) collective-permute-start(f32[34,1]{1,0:T(8,128)S(1)} %get-tuple-element.271), channel_id=1, source_target_pairs={{0,2},{2,4},{4,6},{6,8},{8,10},{10,12},{12,14},{14,16},{16,18},{18... | collective-permute-start | bytes 416 | tf_op jit(solution)/shard_map/ppermute | solution.py:19
  386.3 6.4 %collective-permute-start.13 = (f32[34,1]{1,0:T(8,128)S(1)}, f32[34,1]{1,0:T(8,128)S(1)}, u32[]{:S(2)}, u32[]{:S(2)}) collective-permute-start(f32[34,1]{1,0:T(8,128)S(1)} %get-tuple-element.272), channel_id=1, source_target_pairs={{2,0},{4,2},{6,4},{8,6},{10,8},{12,10},{14,12},{16,14},{18,16},{20... | collective-permute-start | bytes 416 | tf_op jit(solution)/shard_map/ppermute | solution.py:22
  439.8 1.9 collective-permute-start.14
  441.0 3.0 collective-permute-start.15
  444.1 6.0 collective-permute-start.16
  444.1 5.9 collective-permute-start.17
  496.7 2.7 collective-permute-start.18
  498.6 3.0 collective-permute-start.19
  501.7 6.4 %collective-permute-start.20 = (f32[34,1]{1,0:T(8,128)S(1)}, f32[34,1]{1,0:T(8,128)S(1)}, u32[]{:S(2)}, u32[]{:S(2)}) collective-permute-start(f32[34,1]{1,0:T(8,128)S(1)} %get-tuple-element.267), channel_id=1, source_target_pairs={{0,2},{2,4},{4,6},{6,8},{8,10},{10,12},{12,14},{14,16},{16,18},{18... | collective-permute-start | bytes 416 | tf_op jit(solution)/shard_map/ppermute | solution.py:19
  501.8 6.3 %collective-permute-start.21 = (f32[34,1]{1,0:T(8,128)S(1)}, f32[34,1]{1,0:T(8,128)S(1)}, u32[]{:S(2)}, u32[]{:S(2)}) collective-permute-start(f32[34,1]{1,0:T(8,128)S(1)} %get-tuple-element.268), channel_id=1, source_target_pairs={{2,0},{4,2},{6,4},{8,6},{10,8},{12,10},{14,12},{16,14},{18,16},{20... | collective-permute-start | bytes 416 | tf_op jit(solution)/shard_map/ppermute | solution.py:22
  554.2 1.9 collective-permute-start.22
  555.4 3.0 collective-permute-start.23
  558.5 6.0 collective-permute-start.24
  558.6 5.9 collective-permute-start.25
where the time goes:
time: 617 us; the launch traced here: 612 us
  matrix products  225 us (36%)
  blocking collectives  218 us (35%)
  starting transfers between devices  65.9 us (11%)
  waiting for transfers between devices  50.1 us (8%)
  between operations  19.6 us (3%)
  loops' own time  12.5 us (2%)
  other arithmetic  10.9 us (2%)
  local copies, waits for them, and re-layouts  9.98 us (2%)
    dot_general x12, matrix products, spread(): jnp.dot(row_weights, col_weights, precision=lax.Precision.HIGHEST, prefer...  225 us
    psum x20, blocking collectives, by_axis(): value = lax.psum(value, axis)  209 us
    ppermute x12, starting transfers between devices, extended(): lax.ppermute(lax.slice_in_dim(block, 0, width, axis=dim), axis, backward)  28.7 us
    all_to_all x2, waiting for transfers between devices, exchange_both(): tiles = lax.all_to_all(tiles, axis, split_axis=0, concat_axis=0, tiled=True)  24.7 us
    all_to_all x2, starting transfers between devices, exchange_both(): tiles = lax.all_to_all(tiles, axis, split_axis=0, concat_axis=0, tiled=True)  23.8 us
    another operation x1, loops' own time, body(): lax.scan(spread, jnp.zeros((tile_rows + 1, wide), jnp.float32), (scaled_i...  12.5 us
  transfers between devices with their start and end apart: 28, of which 18 were waited for; matrix products, arithmetic and copies ran while one was open for 1% of the time, Pallas kernels for 0%

commit v1 on v0

v1 whole, which is shorter than its diff:
```python
import functools

import jax
import jax.numpy as jnp
from jax import lax
from jax.experimental import pallas as pl
from jax.experimental.pallas import tpu as pltpu
from jax.sharding import PartitionSpec as P

ITERS = 5
CAP = 3
FIELDS = 4
ROWS = CAP * FIELDS
SPLIT = 4
PART = SPLIT + 1
LANE = 128
EDGE = 8
F32 = jnp.float32
BF16 = jnp.bfloat16
MESH = pl.DeviceIdType.MESH
CENTRE = 9.0
RADIUS = 9.0
TRUST = 1000.0


def iota(shape, dim):
    return lax.broadcasted_iota(jnp.int32, shape, dim)


def arrange(tiles, innovation, error, offset, cell, owner, count, send):
    blocks = innovation.shape[0]
    slots = tiles * CAP
    owners = owner[...]
    live = count[0]
    row, col = iota((blocks, blocks), 0), iota((blocks, blocks), 1)
    owners_f = owners.astype(F32)
    owners_col = jnp.sum(jnp.where(row == col, owners_f, 0.0), axis=1, keepdims=True)
    earlier = (owners_col == owners_f) & (row < col) & (row < live)
    rank = jnp.sum(jnp.where(earlier, 1.0, 0.0), axis=0, keepdims=True)
    lane = iota((1, blocks), 1)
    target = jnp.where(lane < live, owners_f * CAP + rank, -1.0)
    pick = jnp.where(iota((slots, blocks), 0).astype(F32) == target, 1.0, 0.0).astype(BF16)
    err = error[...]
    rest = jnp.concatenate(
        [innovation[...] / (err * err), offset[0], offset[1], cell[...].astype(F32)], axis=1
    )
    out = None
    for _ in range(3):
        part = rest.astype(BF16)
        term = jnp.dot(pick, part, preferred_element_type=F32)
        out = term if out is None else out + term
        rest = rest - part.astype(F32)
    for f in range(FIELDS):
        send[pl.ds(f, slots, stride=FIELDS), :] = out[:, f * LANE : (f + 1) * LANE]


def weights_of(values, rows, cols):
    amount, north, east = values[0:1], values[1:2], values[2:3]
    cell = values[3:4].astype(jnp.int32)
    cell_row = cell // cols
    cell_col = cell % cols
    part = cell_col % SPLIT
    spot = iota((8, LANE), 0)
    across = jnp.where(spot == part, 1.0 - east, jnp.where(spot == part + 1, east, 0.0)) * amount
    down_at = iota((rows, LANE), 0)
    down = jnp.where(down_at == cell_row, 1.0 - north, jnp.where(down_at == cell_row + 1, north, 0.0))
    below = jnp.where(cell_row == rows - 1, north, 0.0) * across
    pieces = [down * across[c : c + 1] for c in range(PART)]
    pieces += [below, jnp.zeros((8, LANE), F32)]
    weight = jnp.concatenate(pieces, axis=0)
    hot = jnp.where(iota((cols // SPLIT, LANE), 0) == cell_col // SPLIT, 1.0, 0.0).astype(BF16)
    return weight, hot


def spread_some(values, rows, cols, total):
    sides = [weights_of(values[i : i + FIELDS], rows, cols) for i in range(0, values.shape[0], FIELDS)]
    weight = jnp.concatenate([s[0] for s in sides], axis=1)
    hot = jnp.concatenate([s[1] for s in sides], axis=1)
    high = weight.astype(BF16)
    low = (weight - high.astype(F32)).astype(BF16)
    both = jnp.concatenate([high, low], axis=0)
    total[...] += lax.dot_general(both, hot, (((1,), (1,)), ((), ())), preferred_element_type=F32)


def total_shape(rows, cols):
    return (2 * (PART * rows + 16), cols // SPLIT)


def unpack(total, rows, cols, part):
    wide = cols // SPLIT
    half = rows // 2
    count = PART * rows + 16
    acc = total[0:count, :] + total[count : 2 * count, :]
    under = acc[PART * rows : PART * rows + 8]
    top = iota((8, wide), 0) == 0
    fields = []
    for c in range(PART):
        row = jnp.where(top, jnp.broadcast_to(under[c : c + 1], (8, wide)), 0.0)
        fields.append(jnp.concatenate([acc[c * rows : (c + 1) * rows], row], axis=0))
    carried = pltpu.roll(fields[SPLIT], 1, 1)
    first = iota(carried.shape, 1) == 0
    past = jnp.where(first, carried, 0.0)[:, :LANE]
    fields[0] = fields[0] + jnp.where(first, 0.0, carried)
    size = SPLIT * LANE
    source, place = iota((size, size), 0), iota((size, size), 1)
    order = jnp.where(place == SPLIT * (source % LANE) + source // LANE, 1.0, 0.0).astype(BF16)
    strips = []
    for j in range(wide // LANE):
        rest = jnp.concatenate([f[:, j * LANE : (j + 1) * LANE] for f in fields[:SPLIT]], axis=1)
        out = None
        for _ in range(3):
            piece = rest.astype(BF16)
            term = jnp.dot(piece, order, preferred_element_type=F32)
            out = term if out is None else out + term
            rest = rest - piece.astype(F32)
        strips.append(out)
    for j, out in enumerate(strips):
        at = slice(j * size, (j + 1) * size)
        part[0, 0:half, at] = out[0:half]
        part[0, half : half + 8, at] = jnp.zeros((8, size), F32)
        part[1, :, at] = out[half:]
    part[0, 0:half, cols:] = past[0:half]
    part[0, half : half + 8, cols:] = jnp.zeros((8, LANE), F32)
    part[1, :, cols:] = past[half:]


def spread_kernel(rows, cols, recv, part, total):
    total[...] = jnp.zeros_like(total)
    step = 2 * ROWS

    def some(i, carry):
        spread_some(recv[pl.ds(pl.multiple_of(i * step, 8), step), :], rows, cols, total)
        return carry

    lax.fori_loop(0, recv.shape[0] // step, some, 0)
    unpack(total, rows, cols, part)


def add_up(values):
    while len(values) > 1:
        rest = values[len(values) & ~1 :]
        values = [values[i] + values[i + 1] for i in range(0, len(values) - 1, 2)] + rest
    return values[0]


def coefficients(mu):
    start = mu[0]
    mu = [m / start for m in mu]
    gram = {}
    for s in range(2 * ITERS + 1):
        for d in range(s + 1):
            gram[s, d] = 0.5 * (mu[s] + mu[d])

    def inner(a, b):
        terms = [a[i] * b[j] * gram[i + j, abs(i - j)] for i in range(len(a)) for j in range(len(b))]
        return add_up(terms)

    def operate(a):
        out = [CENTRE * v for v in a] + [None]
        for i, v in enumerate(a):
            for j, f in ((1, RADIUS),) if i == 0 else ((i + 1, RADIUS / 2), (i - 1, RADIUS / 2)):
                out[j] = f * v if out[j] is None else out[j] + f * v
        return out

    one = jnp.ones_like(start)
    field, residual, direction = [], [one], [one]
    norm = one
    worst = one
    for _ in range(ITERS):
        applied = operate(direction)
        step = norm / inner(direction, applied)
        field = [
            step * d + (field[i] if i < len(field) else 0.0) for i, d in enumerate(direction)
        ]
        residual = [
            (residual[i] if i < len(residual) else 0.0) - step * a for i, a in enumerate(applied)
        ]
        after = inner(residual, residual)
        size = add_up([jnp.abs(v) for v in residual])
        worst = jnp.maximum(worst, jnp.where(after > 0, size * size / after, 1e30))
        ratio = after / norm
        direction = [
            v + (ratio * direction[i] if i < len(direction) else 0.0) for i, v in enumerate(residual)
        ]
        norm = after
    sound = jnp.where(worst < TRUST, 1.0, 0.0)
    return field, residual, sound


def solve_kernel(
    n_lat,
    n_lon,
    part,
    land,
    inertia,
    depth,
    field_out,
    residual_out,
    forcing_out,
    sound_out,
    got,
    mine,
    west,
    east,
    tall,
    above,
    below,
    coef,
    cond,
    basis,
    line_in,
    line_at,
    rank_in,
    rank_at,
    send_sem,
    recv_sem,
    line_send,
    line_recv,
    rank_send,
    rank_recv,
):
    rows, cols = land.shape
    high, wide = rows + 2 * EDGE, cols + 2 * LANE
    lat, lon, obs = lax.axis_index("lat"), lax.axis_index("lon"), lax.axis_index("obs")
    ranks = 2 * n_lat
    rank = lat * 2 + obs

    def on_line(k):
        return {"lon": k}

    def on_rank(k):
        return {"lat": k // 2, "obs": k % 2}

    barrier = pltpu.get_barrier_semaphore()

    def greet_line(d, carry):
        pl.semaphore_signal(barrier, 1, device_id=on_line((lon + d) % n_lon), device_id_type=MESH)
        return carry

    def greet_rank(d, carry):
        pl.semaphore_signal(barrier, 1, device_id=on_rank((rank + d) % ranks), device_id_type=MESH)
        return carry

    lax.fori_loop(1, n_lon, greet_line, 0)
    lax.fori_loop(1, ranks, greet_rank, 0)

    inner_rows, inner_cols = slice(EDGE, EDGE + rows), slice(LANE, LANE + cols)
    coef[0, inner_rows, inner_cols] = land[...].astype(F32) * depth[...]
    coef[1, inner_rows, inner_cols] = inertia[...]
    pl.semaphore_wait(barrier, n_lon - 1 + ranks - 1)

    def copy(k, src, dst, device):
        c = pltpu.make_async_remote_copy(
            src_ref=src,
            dst_ref=dst,
            send_sem=send_sem.at[k],
            recv_sem=recv_sem.at[k],
            device_id=device,
            device_id_type=MESH,
        )
        c.start()
        return c

    to_east, to_west = on_line((lon + 1) % n_lon), on_line((lon + n_lon - 1) % n_lon)
    to_south, to_north = on_rank((rank + 1) % ranks), on_rank((rank + ranks - 1) % ranks)
    own = pl.ds(EDGE, rows)

    pair = copy(0, part.at[1 - obs], got, {"obs": 1 - obs})
    coef_e = copy(1, coef.at[:, own, pl.ds(cols, LANE)], coef.at[:, own, pl.ds(0, LANE)], to_east)
    coef_w = copy(2, coef.at[:, own, pl.ds(LANE, LANE)], coef.at[:, own, pl.ds(LANE + cols, LANE)], to_west)
    pair.wait_recv()
    mine[...] = part[obs] + got[...]
    mine_e = copy(3, mine.at[:, pl.ds(cols - LANE, 2 * LANE)], west, to_east)
    mine_w = copy(4, mine.at[:, pl.ds(0, LANE)], east, to_west)
    coef_e.wait_recv()
    coef_w.wait_recv()
    coef_s = copy(5, coef.at[:, pl.ds(rows, EDGE), :], coef.at[:, pl.ds(0, EDGE), :], to_south)
    coef_n = copy(6, coef.at[:, pl.ds(EDGE, EDGE), :], coef.at[:, pl.ds(EDGE + rows, EDGE), :], to_north)
    mine_e.wait_recv()
    mine_w.wait_recv()
    tall[:, 0:LANE] = west[:, 0:LANE]
    tall[:, LANE : 2 * LANE] = mine[:, 0:LANE] + west[:, LANE:]
    tall[:, 2 * LANE : LANE + cols] = mine[:, LANE:cols]
    tall[:, LANE + cols :] = mine[:, cols:] + east[...]
    tall_s = copy(7, tall.at[pl.ds(rows - EDGE, 2 * EDGE), :], above, to_south)
    tall_n = copy(8, tall.at[pl.ds(0, EDGE), :], below, to_north)
    coef_s.wait_recv()
    coef_n.wait_recv()
    conduct = coef[0]
    north = jnp.sqrt(conduct * pltpu.roll(conduct, 1, 0))
    south = pltpu.roll(north, high - 1, 0)
    left = jnp.sqrt(conduct * pltpu.roll(conduct, 1, 1))
    right = pltpu.roll(left, wide - 1, 1)
    cond[0] = (coef[1] + north + south + left + right - CENTRE) * (1.0 / RADIUS)
    cond[1] = north * (1.0 / RADIUS)
    cond[2] = south * (1.0 / RADIUS)
    cond[3] = left * (1.0 / RADIUS)
    cond[4] = right * (1.0 / RADIUS)
    tall_s.wait_recv()
    tall_n.wait_recv()
    ocean = coef[0] > 0
    raw = jnp.concatenate(
        [
            above[0:EDGE, :],
            tall[0:EDGE, :] + above[EDGE:, :],
            tall[EDGE:rows, :],
            below[...] + tall[rows:, :],
        ],
        axis=0,
    )
    basis[0] = jnp.where(ocean, raw, 0.0)
    forcing_out[...] = basis[0, inner_rows, inner_cols]

    def operate(v):
        return (
            cond[0] * v
            - cond[1] * pltpu.roll(v, 1, 0)
            - cond[2] * pltpu.roll(v, high - 1, 0)
            - cond[3] * pltpu.roll(v, 1, 1)
            - cond[4] * pltpu.roll(v, wide - 1, 1)
        )

    for k in range(ITERS):
        after = operate(basis[k])
        basis[k + 1] = after if k == 0 else 2.0 * after - basis[k - 1]

    def dot(i, j):
        pieces = []
        for a in range(EDGE, EDGE + rows, 8):
            for b in range(LANE, LANE + cols, LANE):
                pieces.append(basis[i, a : a + 8, b : b + LANE] * basis[j, a : a + 8, b : b + LANE])
        return jnp.sum(add_up(pieces), axis=0, keepdims=True)

    pairs = [(k // 2, (k + 1) // 2) for k in range(2 * ITERS + 1)]
    sums = [dot(i, j) for i, j in pairs]
    stack = jnp.concatenate(sums + [jnp.zeros((16 - len(sums), LANE), F32)], axis=0)
    column = jnp.sum(stack, axis=1, keepdims=True)
    diag = iota((16, LANE), 0) == iota((16, LANE), 1)
    line_in[...] = jnp.sum(jnp.where(diag, column, 0.0), axis=0, keepdims=True)

    def share(count, me, device, value, at, s_sem, r_sem):
        def copy_of(slot, k, target):
            return pltpu.make_async_remote_copy(
                src_ref=value,
                dst_ref=at.at[slot],
                send_sem=s_sem.at[k],
                recv_sem=r_sem.at[slot],
                device_id=device(target),
                device_id_type=MESH,
            )

        def begin(d, carry):
            copy_of(me, d, (me + d) % count).start()
            return carry

        def arrive(d, carry):
            copy_of((me + count - d) % count, d, (me + d) % count).wait_recv()
            return carry

        def leave(d, carry):
            copy_of(me, d, (me + d) % count).wait_send()
            return carry

        lax.fori_loop(1, count, begin, 0)
        at[me] = value[...]
        lax.fori_loop(1, count, arrive, 0)
        lax.fori_loop(1, count, leave, 0)
        return add_up([at[k] for k in range(count)])

    rank_in[...] = share(n_lon, lon, on_line, line_in, line_at, line_send, line_recv)
    sums = share(ranks, rank, on_rank, rank_in, rank_at, rank_send, rank_recv)
    lane = iota((1, LANE), 1)
    raw_sums = [
        jnp.sum(jnp.where(lane == k, sums, 0.0), axis=1, keepdims=True) for k in range(2 * ITERS + 1)
    ]
    mu = [
        raw_sums[k] if k < 2 else 2.0 * raw_sums[k] - raw_sums[k % 2] for k in range(2 * ITERS + 1)
    ]
    field, residual, sound = coefficients(mu)
    views = [basis[k, inner_rows, inner_cols] for k in range(ITERS + 1)]
    field_out[...] = add_up([c * v for c, v in zip(field, views)])
    residual_out[...] = add_up([c * v for c, v in zip(residual, views)])
    sound_out[...] = jnp.broadcast_to(sound, (1, LANE))
    for c in (pair, coef_e, coef_w, mine_e, mine_w, coef_s, coef_n, tall_s, tall_n):
        c.wait_send()


def solve(n_lat, n_lon, part, land, inertia, depth):
    rows, cols = land.shape
    high, wide = rows + 2 * EDGE, cols + 2 * LANE
    own = jax.ShapeDtypeStruct((rows, cols), F32)
    vmem = pl.BlockSpec(memory_space=pltpu.VMEM)
    ranks = 2 * n_lat
    return pl.pallas_call(
        functools.partial(solve_kernel, n_lat, n_lon),
        out_shape=(own, own, own, jax.ShapeDtypeStruct((1, LANE), F32)),
        in_specs=[vmem] * 4,
        out_specs=(vmem,) * 4,
        scratch_shapes=[
            pltpu.VMEM((rows + EDGE, cols + LANE), F32),
            pltpu.VMEM((rows + EDGE, cols + LANE), F32),
            pltpu.VMEM((rows + EDGE, 2 * LANE), F32),
            pltpu.VMEM((rows + EDGE, LANE), F32),
            pltpu.VMEM((rows + EDGE, wide), F32),
            pltpu.VMEM((2 * EDGE, wide), F32),
            pltpu.VMEM((EDGE, wide), F32),
            pltpu.VMEM((2, high, wide), F32),
            pltpu.VMEM((5, high, wide), F32),
            pltpu.VMEM((ITERS + 1, high, wide), F32),
            pltpu.VMEM((1, LANE), F32),
            pltpu.VMEM((n_lon, 1, LANE), F32),
            pltpu.VMEM((1, LANE), F32),
            pltpu.VMEM((ranks, 1, LANE), F32),
            pltpu.SemaphoreType.DMA((9,)),
            pltpu.SemaphoreType.DMA((9,)),
            pltpu.SemaphoreType.DMA((n_lon,)),
            pltpu.SemaphoreType.DMA((n_lon,)),
            pltpu.SemaphoreType.DMA((ranks,)),
            pltpu.SemaphoreType.DMA((ranks,)),
        ],
        compiler_params=pltpu.CompilerParams(collective_id=1, has_side_effects=True),
    )(part, land, inertia, depth)


def shifted(value, axis, steps):
    count = lax.axis_size(axis)
    return lax.ppermute(value, axis, [(i, (i + steps) % count) for i in range(count)])


def border(block):
    for axis, dim in ((("lat", "obs"), 0), ("lon", 1)):
        size = block.shape[dim]
        low = shifted(lax.slice_in_dim(block, size - 1, size, axis=dim), axis, 1)
        high = shifted(lax.slice_in_dim(block, 0, 1, axis=dim), axis, -1)
        block = jnp.concatenate([low, block, high], axis=dim)
    return block


def stepwise(forcing, land, inertia, depth):
    conduct = land.astype(F32) * depth
    padded = border(conduct)
    north = jnp.sqrt(conduct * padded[:-2, 1:-1])
    south = jnp.sqrt(conduct * padded[2:, 1:-1])
    west = jnp.sqrt(conduct * padded[1:-1, :-2])
    east = jnp.sqrt(conduct * padded[1:-1, 2:])
    diagonal = inertia + north + south + west + east

    def whole(value):
        return lax.psum(jnp.sum(value), ("lat", "lon", "obs"))

    def step(_, state):
        field, residual, direction, norm = state
        outer = border(direction)
        applied = (
            diagonal * direction
            - north * outer[:-2, 1:-1]
            - south * outer[2:, 1:-1]
            - west * outer[1:-1, :-2]
            - east * outer[1:-1, 2:]
        )
        size = norm / whole(direction * applied)
        field = field + size * direction
        residual = residual - size * applied
        after = whole(residual * residual)
        return field, residual, residual + after / norm * direction, after

    state = (jnp.zeros_like(forcing), forcing, forcing, whole(forcing * forcing))
    return lax.fori_loop(0, ITERS, step, state)[:2]


def body(n_lat, n_lon, innovation, error, offset, cell, owner, count, land, inertia, depth):
    tiles = n_lat * n_lon
    rows, cols = 2 * land.shape[0], land.shape[1]
    vmem = pl.BlockSpec(memory_space=pltpu.VMEM)
    send = pl.pallas_call(
        functools.partial(arrange, tiles),
        out_shape=jax.ShapeDtypeStruct((tiles * ROWS, LANE), F32),
        in_specs=[vmem] * 5 + [pl.BlockSpec(memory_space=pltpu.SMEM)],
        out_specs=vmem,
    )(innovation, error, offset, cell, owner, count)
    recv = lax.all_to_all(
        send.reshape(tiles, ROWS, LANE), ("lat", "lon"), split_axis=0, concat_axis=0, tiled=True
    ).reshape(tiles * ROWS, LANE)
    part = pl.pallas_call(
        functools.partial(spread_kernel, rows, cols),
        out_shape=jax.ShapeDtypeStruct((2, rows // 2 + EDGE, cols + LANE), F32),
        in_specs=[vmem],
        out_specs=vmem,
        scratch_shapes=[pltpu.VMEM(total_shape(rows, cols), F32)],
    )(recv)
    field, residual, forcing, sound = solve(n_lat, n_lon, part, land, inertia, depth)
    return lax.cond(
        sound[0, 0] > 0.5,
        lambda: (field, residual),
        lambda: stepwise(forcing, land, inertia, depth),
    )


def solution(mesh):
    split = ("lat", "lon", "obs")
    grid = P(("lat", "obs"), "lon")
    return jax.shard_map(
        functools.partial(body, mesh.shape["lat"], mesh.shape["lon"]),
        mesh=mesh,
        in_specs=(
            P(split, None),
            P(split, None),
            P(None, split, None),
            P(split, None),
            P(split, None),
            P(split),
            grid,
            grid,
            grid,
        ),
        out_specs=(grid, grid),
        check_vma=False,
    )
```

time: 617 us -> 117 us (0.19)
  matrix products: 225 us -> 0 us
  blocking collectives: 218 us -> 44.9 us
  starting transfers between devices: 65.9 us -> 0 us
  Pallas kernels: 0 us -> 65 us
  waiting for transfers between devices: 50.1 us -> 0 us
  between operations: 19.6 us -> 1.36 us
  loops' own time: 12.5 us -> 0.24 us
  other arithmetic: 10.9 us -> 0 us
    dot_general x12 -> x0, matrix products: 225 us -> none  [spread(): jnp.dot(row_weights, col_weights, precision=lax.Precision.HIGHEST, prefer...]
    psum x20 -> x0, blocking collectives: 209 us -> none  [by_axis(): value = lax.psum(value, axis)]
    pallas_call x0 -> x3, Pallas kernels: none -> 65 us  [the longest x1 36.2 us: body(): pl.pallas_call(functools.partial(spread_kernel, rows, cols), out_shape=ja...]
    ppermute x26 -> x0, starting transfers between devices: 42 us -> none  [the longest x12 28.7 us: extended(): lax.ppermute(lax.slice_in_dim(block, 0, width, axis=dim), axis, backward)]
    all_to_all x1, blocking collectives: 9.09 us -> 44.9 us  [body(): lax.all_to_all(send.reshape(tiles, ROWS, LANE), ('lat', 'lon'), split_axi...]
    ppermute x26 -> x0, waiting for transfers between devices: 25.4 us -> none  [the longest x12 10.4 us: extended(): lax.ppermute(lax.slice_in_dim(block, 0, width, axis=dim), axis, backward)]
    all_to_all x2 -> x0, waiting for transfers between devices: 24.7 us -> none  [exchange_both(): tiles = lax.all_to_all(tiles, axis, split_axis=0, concat_axis=0, tiled=True)]
    all_to_all x2 -> x0, starting transfers between devices: 23.8 us -> none  [exchange_both(): tiles = lax.all_to_all(tiles, axis, split_axis=0, concat_axis=0, tiled=True)]
  transfers between devices with their start and end apart: 28 -> 0, of which waited for: 18 -> 0; matrix products, arithmetic and copies ran while one was open for 1% -> 0% of each run, Pallas kernels for 0% -> 0%
where the time goes in v1:
time: 117 us; the launch traced here: 116 us
  Pallas kernels  65 us (56%)
  blocking collectives  44.9 us (38%)
  local copies, waits for them, and re-layouts  5.05 us (4%)
  between operations  1.36 us (1%)
    all_to_all x1, blocking collectives, body(): lax.all_to_all(send.reshape(tiles, ROWS, LANE), ('lat', 'lon'), split_axi...  44.9 us
    pallas_call x1, Pallas kernels, body(): pl.pallas_call(functools.partial(spread_kernel, rows, cols), out_shape=ja...  36.2 us
    pallas_call x1, Pallas kernels, solve(): pl.pallas_call(functools.partial(solve_kernel, n_lat, n_lon), out_shape=(...  26.4 us
    unnamed x10, local copies, waits for them, and re-layouts  2.89 us
    pallas_call x1, Pallas kernels, body(): pl.pallas_call(functools.partial(arrange, tiles), out_shape=jax.ShapeDtyp...  2.43 us

profile of v1, /device:TPU:1, one launch (start us, length us, event | category | flops | bytes accessed | tf_op | source)
XLA Modules:
  0.0 116.5 jit_solution(18167949469012866148)
XLA Ops:
  1.3 2.4 %shard_map.104 = f32[1536,128]{1,0:T(8,128)} custom-call(f32[128,128]{1,0:T(8,128)} %innovation.1, f32[128,128]{1,0:T(8,128)} %error.1, f32[2,128,128]{2,1,0:T(8,128)} %offset.1, s32[128,128]{1,0:T(8,128)} %cell.1, s32[1,128]{1,0:T(1,128)} %owner.1, s32[1]{0:T(128)S(6)} %copy.32.count), custom_call_target="tpu_custom_call" | custom-call | tf_op jit(solution)/shard_map/pallas_call | solution.py:475
  3.7 1.2 %reshape.14 = f32[128,12,128]{2,1,0:T(8,128)S(1)} reshape(f32[1536,128]{1,0:T(8,128)} %shard_map.104) | data formatting | bytes 1572864 | tf_op jit(solution)/shard_map/reshape | solution.py:482
  4.9 44.9 %all_to_all.5 = f32[128,12,128]{2,1,0:T(8,128)S(1)} all-to-all(f32[128,12,128]{2,1,0:T(8,128)S(1)} %reshape.14), channel_id=1, replica_groups=mesh['lat'=8,'lon'=16,'obs'=2] {'lat','lon'}, dimensions={0} | all-to-all | bytes 1572864 | tf_op jit(solution)/shard_map/all_to_all | solution.py:481
  49.8 0.9 reshape.15.recv
  50.7 0.0 copy-start
  50.7 0.0 copy-start.1
  50.7 0.0 copy-start.2
  50.7 36.2 %shard_map.105.part = f32[2,40,1152]{2,1,0:T(8,128)} custom-call(f32[1536,128]{1,0:T(8,128)} %reshape.15.recv), custom_call_target="tpu_custom_call" | custom-call | tf_op jit(solution)/shard_map/pallas_call | solution.py:484
  86.9 0.0 copy-done
  86.9 0.0 copy-done.1
  86.9 0.0 copy-done.2
  86.9 26.4 %shard_map.106 = (f32[32,1024]{1,0:T(8,128)}, f32[32,1024]{1,0:T(8,128)S(1)}, f32[32,1024]{1,0:T(8,128)S(1)}, f32[1,128]{1,0:T(1,128)}) custom-call(f32[2,40,1152]{2,1,0:T(8,128)} %shard_map.105.part, s32[32,1024]{1,0:T(8,128)S(1)} %copy-done, f32[32,1024]{1,0:T(8,128)S(1)} %copy-done.2, f32[32,1024]{1,0:T(8,128)S(1)} %copy-done.1), custom_call_target="tpu_custom_call" | custom-call | tf_op jit(solution)/shard_map/pallas_call | solution.py:394
  113.3 0.0 copy-start.3
  113.3 0.7 copy-done.3
  114.0 0.2 conditional.1
  114.2 1.6 %copy.33 = f32[32,1024]{1,0:T(8,128)} copy(f32[32,1024]{1,0:T(8,128)} %get-tuple-element.274) | data formatting | bytes 262144
  115.8 0.7 copy.34
  (1 shorter events, 0.0 us)
Async XLA Ops:
  50.7 36.2 %copy-start = (s32[32,1024]{1,0:T(8,128)S(1)}, s32[32,1024]{1,0:T(8,128)}, u32[]{:S(2)}) copy-start(s32[32,1024]{1,0:T(8,128)} %land.1) | copy-start | bytes 393220
  50.7 36.2 %copy-start.1 = (f32[32,1024]{1,0:T(8,128)S(1)}, f32[32,1024]{1,0:T(8,128)}, u32[]{:S(2)}) copy-start(f32[32,1024]{1,0:T(8,128)} %depth.1) | copy-start | bytes 393220
  50.7 36.2 %copy-start.2 = (f32[32,1024]{1,0:T(8,128)S(1)}, f32[32,1024]{1,0:T(8,128)}, u32[]{:S(2)}) copy-start(f32[32,1024]{1,0:T(8,128)} %inertia.1) | copy-start | bytes 393220
  113.3 0.7 copy-start.3

commit v2 on v1

--- a/solution.py
+++ b/solution.py
@@ -11,6 +11,7 @@
 CAP = 3
 FIELDS = 4
 ROWS = CAP * FIELDS
+GROUP = 4
 SPLIT = 4
 PART = SPLIT + 1
 LANE = 128
@@ -54,7 +55,7 @@
         send[pl.ds(f, slots, stride=FIELDS), :] = out[:, f * LANE : (f + 1) * LANE]
 
 
-def weights_of(values, rows, cols):
+def weigh(values, at, rows, cols, lhs, rhs):
     amount, north, east = values[0:1], values[1:2], values[2:3]
     cell = values[3:4].astype(jnp.int32)
     cell_row = cell // cols
@@ -66,20 +67,30 @@
     down = jnp.where(down_at == cell_row, 1.0 - north, jnp.where(down_at == cell_row + 1, north, 0.0))
     below = jnp.where(cell_row == rows - 1, north, 0.0) * across
     pieces = [down * across[c : c + 1] for c in range(PART)]
-    pieces += [below, jnp.zeros((8, LANE), F32)]
-    weight = jnp.concatenate(pieces, axis=0)
-    hot = jnp.where(iota((cols // SPLIT, LANE), 0) == cell_col // SPLIT, 1.0, 0.0).astype(BF16)
-    return weight, hot
-
-
-def spread_some(values, rows, cols, total):
-    sides = [weights_of(values[i : i + FIELDS], rows, cols) for i in range(0, values.shape[0], FIELDS)]
-    weight = jnp.concatenate([s[0] for s in sides], axis=1)
-    hot = jnp.concatenate([s[1] for s in sides], axis=1)
-    high = weight.astype(BF16)
-    low = (weight - high.astype(F32)).astype(BF16)
-    both = jnp.concatenate([high, low], axis=0)
-    total[...] += lax.dot_general(both, hot, (((1,), (1,)), ((), ())), preferred_element_type=F32)
+    pieces.append(jnp.concatenate([below, jnp.zeros((8, LANE), F32)], axis=0))
+    second = PART * rows + 16
+    lanes = slice(at, at + LANE)
+    for c, piece in enumerate(pieces):
+        high = piece.astype(BF16)
+        low = (piece - high.astype(F32)).astype(BF16)
+        end = c * rows + piece.shape[0]
+        lhs[c * rows : end, lanes] = high
+        lhs[second + c * rows : second + end, lanes] = low
+    hot = jnp.where(iota((cols // SPLIT, LANE), 0) == cell_col // SPLIT, 1.0, 0.0)
+    rhs[:, lanes] = hot.astype(BF16)
+
+
+def weigh_group(recv, start, rows, cols, lhs, rhs):
+    for i in range(0, GROUP * ROWS, 8):
+        pair = recv[pl.ds(pl.multiple_of(start + i, 8), 8), :]
+        for k in range(0, 8, FIELDS):
+            weigh(pair[k : k + FIELDS], (i + k) // FIELDS * LANE, rows, cols, lhs, rhs)
+
+
+def add_group(lhs, rhs, total):
+    total[...] += lax.dot_general(
+        lhs[...], rhs[...], (((1,), (1,)), ((), ())), preferred_element_type=F32
+    )
 
 
 def total_shape(rows, cols):
@@ -124,18 +135,6 @@
     part[1, :, cols:] = past[half:]
 
 
-def spread_kernel(rows, cols, recv, part, total):
-    total[...] = jnp.zeros_like(total)
-    step = 2 * ROWS
-
-    def some(i, carry):
-        spread_some(recv[pl.ds(pl.multiple_of(i * step, 8), step), :], rows, cols, total)
-        return carry
-
-    lax.fori_loop(0, recv.shape[0] // step, some, 0)
-    unpack(total, rows, cols, part)
-
-
 def add_up(values):
     while len(values) > 1:
         rest = values[len(values) & ~1 :]
@@ -187,10 +186,15 @@
     return field, residual, sound
 
 
-def solve_kernel(
+def step_kernel(
     n_lat,
     n_lon,
-    part,
+    innovation,
+    error,
+    offset,
+    cell,
+    owner,
+    count,
     land,
     inertia,
     depth,
@@ -198,6 +202,14 @@
     residual_out,
     forcing_out,
     sound_out,
+    send,
+    recv,
+    lhs_a,
+    rhs_a,
+    lhs_b,
+    rhs_b,
+    total,
+    part,
     got,
     mine,
     west,
@@ -212,6 +224,8 @@
     line_at,
     rank_in,
     rank_at,
+    out_sem,
+    in_sem,
     send_sem,
     recv_sem,
     line_send,
@@ -222,8 +236,11 @@
     rows, cols = land.shape
     high, wide = rows + 2 * EDGE, cols + 2 * LANE
     lat, lon, obs = lax.axis_index("lat"), lax.axis_index("lon"), lax.axis_index("obs")
+    tiles = n_lat * n_lon
     ranks = 2 * n_lat
     rank = lat * 2 + obs
+    quads = n_lon // GROUP
+    groups = n_lat * quads
 
     def on_line(k):
         return {"lon": k}
@@ -231,23 +248,29 @@
     def on_rank(k):
         return {"lat": k // 2, "obs": k % 2}
 
+    def on_tile(k):
+        return {"lat": k // n_lon, "lon": k % n_lon}
+
+    me = lat * n_lon + lon
     barrier = pltpu.get_barrier_semaphore()
 
-    def greet_line(d, carry):
-        pl.semaphore_signal(barrier, 1, device_id=on_line((lon + d) % n_lon), device_id_type=MESH)
+    def greet_tile(d, carry):
+        pl.semaphore_signal(barrier, 1, device_id=on_tile((me + d) % tiles), device_id_type=MESH)
         return carry
 
-    def greet_rank(d, carry):
-        pl.semaphore_signal(barrier, 1, device_id=on_rank((rank + d) % ranks), device_id_type=MESH)
+    def greet_other(d, carry):
+        device = {"lat": (lat + d) % n_lat, "obs": 1 - obs}
+        pl.semaphore_signal(barrier, 1, device_id=device, device_id_type=MESH)
         return carry
 
-    lax.fori_loop(1, n_lon, greet_line, 0)
-    lax.fori_loop(1, ranks, greet_rank, 0)
+    lax.fori_loop(1, tiles, greet_tile, 0)
+    lax.fori_loop(0, n_lat, greet_other, 0)
 
     inner_rows, inner_cols = slice(EDGE, EDGE + rows), slice(LANE, LANE + cols)
     coef[0, inner_rows, inner_cols] = land[...].astype(F32) * depth[...]
     coef[1, inner_rows, inner_cols] = inertia[...]
-    pl.semaphore_wait(barrier, n_lon - 1 + ranks - 1)
+    arrange(tiles, innovation, error, offset, cell, owner, count, send)
+    pl.semaphore_wait(barrier, tiles - 1 + n_lat)
 
     def copy(k, src, dst, device):
         c = pltpu.make_async_remote_copy(
@@ -265,17 +288,82 @@
     to_south, to_north = on_rank((rank + 1) % ranks), on_rank((rank + ranks - 1) % ranks)
     own = pl.ds(EDGE, rows)
 
-    pair = copy(0, part.at[1 - obs], got, {"obs": 1 - obs})
     coef_e = copy(1, coef.at[:, own, pl.ds(cols, LANE)], coef.at[:, own, pl.ds(0, LANE)], to_east)
     coef_w = copy(2, coef.at[:, own, pl.ds(LANE, LANE)], coef.at[:, own, pl.ds(LANE + cols, LANE)], to_west)
+
+    def away(t):
+        j = t // quads
+        return (j % 2) * ((j + 1) // 2) + (1 - j % 2) * (n_lat - j // 2)
+
+    def rows_of(k):
+        return pl.ds(k * ROWS, ROWS)
+
+    my_group = lat * quads + lon // GROUP
+
+    def deliver(n, carry):
+        t, d = n // GROUP, n % GROUP
+        to_lat = (lat + n_lat - away(t) % n_lat) % n_lat
+        to_quad = (lon // GROUP + quads - t % quads) % quads
+        target = to_lat * n_lon + to_quad * GROUP + (lon + d) % GROUP
+        pltpu.make_async_remote_copy(
+            src_ref=send.at[rows_of(target), :],
+            dst_ref=recv.at[rows_of(me), :],
+            send_sem=out_sem,
+            recv_sem=in_sem.at[my_group],
+            device_id=on_tile(target),
+            device_id_type=MESH,
+        ).start()
+        return carry
+
+    pltpu.make_async_copy(send.at[rows_of(me), :], recv.at[rows_of(me), :], in_sem.at[my_group]).start()
+    lax.fori_loop(1, tiles, deliver, 0)
+    total[...] = jnp.zeros_like(total)
+    height = GROUP * ROWS
+
+    def group_of(t):
+        from_lat = (lat + away(t)) % n_lat
+        from_quad = (lon // GROUP + t % quads) % quads
+        return from_lat * quads + from_quad
+
+    def await_group(t):
+        g = group_of(t)
+        landed = recv.at[pl.ds(pl.multiple_of(g * height, 8), height), :]
+        pltpu.make_async_copy(landed, landed, in_sem.at[g]).wait()
+
+    def weigh_next(t, lhs, rhs):
+        weigh_group(recv, group_of(t) * height, 2 * rows, cols, lhs, rhs)
+
+    await_group(0)
+    weigh_next(0, lhs_a, rhs_a)
+
+    def spread_two(i, carry):
+        await_group(2 * i + 1)
+        weigh_next(2 * i + 1, lhs_b, rhs_b)
+        add_group(lhs_a, rhs_a, total)
+        following = jnp.minimum(2 * i + 2, groups - 1)
+
+        @pl.when(i < groups // 2 - 1)
+        def _():
+            await_group(following)
+
+        weigh_next(following, lhs_a, rhs_a)
+        add_group(lhs_b, rhs_b, total)
+        return carry
+
+    lax.fori_loop(0, groups // 2, spread_two, 0)
+    gone = send.at[pl.ds(0, (tiles - 1) * ROWS), :]
+    pltpu.make_async_copy(gone, gone, out_sem).wait()
+    unpack(total, 2 * rows, cols, part)
+
+    coef_e.wait_recv()
+    coef_w.wait_recv()
+    coef_s = copy(5, coef.at[:, pl.ds(rows, EDGE), :], coef.at[:, pl.ds(0, EDGE), :], to_south)
+    coef_n = copy(6, coef.at[:, pl.ds(EDGE, EDGE), :], coef.at[:, pl.ds(EDGE + rows, EDGE), :], to_north)
+    pair = copy(0, part.at[1 - obs], got, {"obs": 1 - obs})
     pair.wait_recv()
     mine[...] = part[obs] + got[...]
     mine_e = copy(3, mine.at[:, pl.ds(cols - LANE, 2 * LANE)], west, to_east)
     mine_w = copy(4, mine.at[:, pl.ds(0, LANE)], east, to_west)
-    coef_e.wait_recv()
-    coef_w.wait_recv()
-    coef_s = copy(5, coef.at[:, pl.ds(rows, EDGE), :], coef.at[:, pl.ds(0, EDGE), :], to_south)
-    coef_n = copy(6, coef.at[:, pl.ds(EDGE, EDGE), :], coef.at[:, pl.ds(EDGE + rows, EDGE), :], to_north)
     mine_e.wait_recv()
     mine_w.wait_recv()
     tall[:, 0:LANE] = west[:, 0:LANE]
@@ -385,18 +473,30 @@
         c.wait_send()
 
 
-def solve(n_lat, n_lon, part, land, inertia, depth):
+def step(n_lat, n_lon, innovation, error, offset, cell, owner, count, land, inertia, depth):
     rows, cols = land.shape
     high, wide = rows + 2 * EDGE, cols + 2 * LANE
     own = jax.ShapeDtypeStruct((rows, cols), F32)
     vmem = pl.BlockSpec(memory_space=pltpu.VMEM)
     ranks = 2 * n_lat
+    tiles = n_lat * n_lon
+    groups = tiles // GROUP
+    tall = total_shape(2 * rows, cols)
+    deep = GROUP * CAP * LANE
     return pl.pallas_call(
-        functools.partial(solve_kernel, n_lat, n_lon),
+        functools.partial(step_kernel, n_lat, n_lon),
         out_shape=(own, own, own, jax.ShapeDtypeStruct((1, LANE), F32)),
-        in_specs=[vmem] * 4,
+        in_specs=[vmem] * 5 + [pl.BlockSpec(memory_space=pltpu.SMEM)] + [vmem] * 3,
         out_specs=(vmem,) * 4,
         scratch_shapes=[
+            pltpu.VMEM((tiles * ROWS, LANE), F32),
+            pltpu.VMEM((tiles * ROWS, LANE), F32),
+            pltpu.VMEM((tall[0], deep), BF16),
+            pltpu.VMEM((tall[1], deep), BF16),
+            pltpu.VMEM((tall[0], deep), BF16),
+            pltpu.VMEM((tall[1], deep), BF16),
+            pltpu.VMEM(tall, F32),
+            pltpu.VMEM((2, rows + EDGE, cols + LANE), F32),
             pltpu.VMEM((rows + EDGE, cols + LANE), F32),
             pltpu.VMEM((rows + EDGE, cols + LANE), F32),
             pltpu.VMEM((rows + EDGE, 2 * LANE), F32),
@@ -411,6 +511,8 @@
             pltpu.VMEM((n_lon, 1, LANE), F32),
             pltpu.VMEM((1, LANE), F32),
             pltpu.VMEM((ranks, 1, LANE), F32),
+            pltpu.SemaphoreType.DMA,
+            pltpu.SemaphoreType.DMA((groups,)),
             pltpu.SemaphoreType.DMA((9,)),
             pltpu.SemaphoreType.DMA((9,)),
             pltpu.SemaphoreType.DMA((n_lon,)),
@@ -419,7 +521,7 @@
             pltpu.SemaphoreType.DMA((ranks,)),
         ],
         compiler_params=pltpu.CompilerParams(collective_id=1, has_side_effects=True),
-    )(part, land, inertia, depth)
+    )(innovation, error, offset, cell, owner, count, land, inertia, depth)
 
 
 def shifted(value, axis, steps):
@@ -468,27 +570,9 @@
     return lax.fori_loop(0, ITERS, step, state)[:2]
 
 
-def body(n_lat, n_lon, innovation, error, offset, cell, owner, count, land, inertia, depth):
-    tiles = n_lat * n_lon
-    rows, cols = 2 * land.shape[0], land.shape[1]
-    vmem = pl.BlockSpec(memory_space=pltpu.VMEM)
-    send = pl.pallas_call(
-        functools.partial(arrange, tiles),
-        out_shape=jax.ShapeDtypeStruct((tiles * ROWS, LANE), F32),
-        in_specs=[vmem] * 5 + [pl.BlockSpec(memory_space=pltpu.SMEM)],
-        out_specs=vmem,
-    )(innovation, error, offset, cell, owner, count)
-    recv = lax.all_to_all(
-        send.reshape(tiles, ROWS, LANE), ("lat", "lon"), split_axis=0, concat_axis=0, tiled=True
-    ).reshape(tiles * ROWS, LANE)
-    part = pl.pallas_call(
-        functools.partial(spread_kernel, rows, cols),
-        out_shape=jax.ShapeDtypeStruct((2, rows // 2 + EDGE, cols + LANE), F32),
-        in_specs=[vmem],
-        out_specs=vmem,
-        scratch_shapes=[pltpu.VMEM(total_shape(rows, cols), F32)],
-    )(recv)
-    field, residual, forcing, sound = solve(n_lat, n_lon, part, land, inertia, depth)
+def body(n_lat, n_lon, *inputs):
+    land, inertia, depth = inputs[-3:]
+    field, residual, forcing, sound = step(n_lat, n_lon, *inputs)
     return lax.cond(
         sound[0, 0] > 0.5,
         lambda: (field, residual),

time: 117 us -> 95.2 us (0.81)
  blocking collectives: 44.9 us -> 0 us
  Pallas kernels: 65 us -> 90.5 us
  local copies, waits for them, and re-layouts: 5.05 us -> 2.9 us
    all_to_all x1 -> x0, blocking collectives: 44.9 us -> none  [body(): lax.all_to_all(send.reshape(tiles, ROWS, LANE), ('lat', 'lon'), split_axi...]
    pallas_call x3 -> x1, Pallas kernels: 65 us -> 90.5 us  [step(): pl.pallas_call(functools.partial(step_kernel, n_lat, n_lon), out_shape=(o...]
    reshape x2 -> x0, local copies, waits for them, and re-layouts: 2.15 us -> none  [the longest x1 1.2 us: body(): send.reshape(tiles, ROWS, LANE)]
where the time goes in v2:
time: 95.2 us; the launch traced here: 95.1 us
  Pallas kernels  90.5 us (95%)
  local copies, waits for them, and re-layouts  2.9 us (3%)
  between operations  1.39 us (1%)
    pallas_call x1, Pallas kernels, step(): pl.pallas_call(functools.partial(step_kernel, n_lat, n_lon), out_shape=(o...  90.5 us
    unnamed x10, local copies, waits for them, and re-layouts  2.89 us

profile of v2, /device:TPU:1, one launch (start us, length us, event | category | flops | bytes accessed | tf_op | source)
XLA Modules:
  0.0 95.1 jit_solution(13949021880256806962)
XLA Ops:
  1.3 0.0 copy-start
  1.3 0.0 copy-start.1
  1.3 0.0 copy-start.2
  1.3 90.5 %shard_map.104 = (f32[32,1024]{1,0:T(8,128)}, f32[32,1024]{1,0:T(8,128)S(1)}, f32[32,1024]{1,0:T(8,128)S(1)}, f32[1,128]{1,0:T(1,128)}) custom-call(f32[128,128]{1,0:T(8,128)} %innovation.1, f32[128,128]{1,0:T(8,128)} %error.1, f32[2,128,128]{2,1,0:T(8,128)} %offset.1, s32[128,128]{1,0:T(8,128)} %cell.1, s32[1,128]{1,0:T(1,128)} %owner.1, s32[1]{0:T(128)S(6)} %copy.32.count, ...), custom_call_target="tpu_custom_call" | custom-call | tf_op jit(solution)/shard_map/pallas_call | solution.py:486
  91.9 0.0 copy-start.3
  91.9 0.7 copy-done.3
  92.6 0.0 copy-done
  92.6 0.0 copy-done.1
  92.6 0.0 copy-done.2
  92.6 0.2 conditional.1
  92.9 1.6 %copy.33 = f32[32,1024]{1,0:T(8,128)} copy(f32[32,1024]{1,0:T(8,128)} %get-tuple-element.274) | data formatting | bytes 262144
  94.4 0.7 copy.34
  (1 shorter events, 0.0 us)
Async XLA Ops:
  1.3 91.3 %copy-start = (s32[32,1024]{1,0:T(8,128)S(1)}, s32[32,1024]{1,0:T(8,128)}, u32[]{:S(2)}) copy-start(s32[32,1024]{1,0:T(8,128)} %land.1) | copy-start | bytes 393220
  1.3 91.3 %copy-start.1 = (f32[32,1024]{1,0:T(8,128)S(1)}, f32[32,1024]{1,0:T(8,128)}, u32[]{:S(2)}) copy-start(f32[32,1024]{1,0:T(8,128)} %depth.1) | copy-start | bytes 393220
  1.3 91.3 %copy-start.2 = (f32[32,1024]{1,0:T(8,128)S(1)}, f32[32,1024]{1,0:T(8,128)}, u32[]{:S(2)}) copy-start(f32[32,1024]{1,0:T(8,128)} %inertia.1) | copy-start | bytes 393220
  91.9 0.7 copy-start.3

commit v3 on v2

--- a/solution.py
+++ b/solution.py
@@ -11,7 +11,7 @@
 CAP = 3
 FIELDS = 4
 ROWS = CAP * FIELDS
-GROUP = 4
+GROUP = 8
 SPLIT = 4
 PART = SPLIT + 1
 LANE = 128
@@ -55,12 +55,12 @@
         send[pl.ds(f, slots, stride=FIELDS), :] = out[:, f * LANE : (f + 1) * LANE]
 
 
-def weigh(values, at, rows, cols, lhs, rhs):
+def weigh(values, k, rows, cols, index, lhs, rhs):
     amount, north, east = values[0:1], values[1:2], values[2:3]
     cell = values[3:4].astype(jnp.int32)
-    cell_row = cell // cols
-    cell_col = cell % cols
-    part = cell_col % SPLIT
+    cell_row = lax.div(cell, cols)
+    cell_col = lax.rem(cell, cols)
+    part = lax.rem(cell_col, SPLIT)
     spot = iota((8, LANE), 0)
     across = jnp.where(spot == part, 1.0 - east, jnp.where(spot == part + 1, east, 0.0)) * amount
     down_at = iota((rows, LANE), 0)
@@ -69,27 +69,29 @@
     pieces = [down * across[c : c + 1] for c in range(PART)]
     pieces.append(jnp.concatenate([below, jnp.zeros((8, LANE), F32)], axis=0))
     second = PART * rows + 16
-    lanes = slice(at, at + LANE)
     for c, piece in enumerate(pieces):
-        high = piece.astype(BF16)
-        low = (piece - high.astype(F32)).astype(BF16)
         end = c * rows + piece.shape[0]
-        lhs[c * rows : end, lanes] = high
-        lhs[second + c * rows : second + end, lanes] = low
-    hot = jnp.where(iota((cols // SPLIT, LANE), 0) == cell_col // SPLIT, 1.0, 0.0)
-    rhs[:, lanes] = hot.astype(BF16)
-
-
-def weigh_group(recv, start, rows, cols, lhs, rhs):
+        main = piece.astype(BF16)
+        lhs[k, c * rows : end, :] = main
+        lhs[k, second + c * rows : second + end, :] = (piece - main.astype(F32)).astype(BF16)
+    spots = index[...]
+    column = lax.div(cell_col, SPLIT).astype(F32).astype(BF16)
+    rhs[k] = jnp.where(spots == column, jnp.ones_like(spots), jnp.zeros_like(spots))
+
+
+def weigh_group(recv, start, rows, cols, index, lhs, rhs):
     for i in range(0, GROUP * ROWS, 8):
         pair = recv[pl.ds(pl.multiple_of(start + i, 8), 8), :]
         for k in range(0, 8, FIELDS):
-            weigh(pair[k : k + FIELDS], (i + k) // FIELDS * LANE, rows, cols, lhs, rhs)
+            weigh(pair[k : k + FIELDS], (i + k) // FIELDS, rows, cols, index, lhs, rhs)
 
 
 def add_group(lhs, rhs, total):
     total[...] += lax.dot_general(
-        lhs[...], rhs[...], (((1,), (1,)), ((), ())), preferred_element_type=F32
+        jnp.concatenate([lhs[k] for k in range(lhs.shape[0])], axis=1),
+        jnp.concatenate([rhs[k] for k in range(rhs.shape[0])], axis=1),
+        (((1,), (1,)), ((), ())),
+        preferred_element_type=F32,
     )
 
 
@@ -208,6 +210,7 @@
     rhs_a,
     lhs_b,
     rhs_b,
+    index,
     total,
     part,
     got,
@@ -246,20 +249,21 @@
         return {"lon": k}
 
     def on_rank(k):
-        return {"lat": k // 2, "obs": k % 2}
+        return {"lat": lax.div(k, 2), "obs": lax.rem(k, 2)}
 
     def on_tile(k):
-        return {"lat": k // n_lon, "lon": k % n_lon}
+        return {"lat": lax.div(k, n_lon), "lon": lax.rem(k, n_lon)}
 
     me = lat * n_lon + lon
     barrier = pltpu.get_barrier_semaphore()
 
     def greet_tile(d, carry):
-        pl.semaphore_signal(barrier, 1, device_id=on_tile((me + d) % tiles), device_id_type=MESH)
+        device = on_tile(lax.rem(me + d, tiles))
+        pl.semaphore_signal(barrier, 1, device_id=device, device_id_type=MESH)
         return carry
 
     def greet_other(d, carry):
-        device = {"lat": (lat + d) % n_lat, "obs": 1 - obs}
+        device = {"lat": lax.rem(lat + d, n_lat), "obs": 1 - obs}
         pl.semaphore_signal(barrier, 1, device_id=device, device_id_type=MESH)
         return carry
 
@@ -284,46 +288,53 @@
         c.start()
         return c
 
-    to_east, to_west = on_line((lon + 1) % n_lon), on_line((lon + n_lon - 1) % n_lon)
-    to_south, to_north = on_rank((rank + 1) % ranks), on_rank((rank + ranks - 1) % ranks)
+    to_east, to_west = on_line(lax.rem(lon + 1, n_lon)), on_line(lax.rem(lon + n_lon - 1, n_lon))
+    to_south, to_north = on_rank(lax.rem(rank + 1, ranks)), on_rank(lax.rem(rank + ranks - 1, ranks))
     own = pl.ds(EDGE, rows)
 
     coef_e = copy(1, coef.at[:, own, pl.ds(cols, LANE)], coef.at[:, own, pl.ds(0, LANE)], to_east)
     coef_w = copy(2, coef.at[:, own, pl.ds(LANE, LANE)], coef.at[:, own, pl.ds(LANE + cols, LANE)], to_west)
 
+    quad, place = lax.div(lon, GROUP), lax.rem(lon, GROUP)
+
     def away(t):
-        j = t // quads
-        return (j % 2) * ((j + 1) // 2) + (1 - j % 2) * (n_lat - j // 2)
+        j = lax.div(t, quads)
+        odd = lax.rem(j, 2)
+        return lax.rem(odd * lax.div(j + 1, 2) + (1 - odd) * (n_lat - lax.div(j, 2)), n_lat)
 
     def rows_of(k):
         return pl.ds(k * ROWS, ROWS)
 
-    my_group = lat * quads + lon // GROUP
-
-    def deliver(n, carry):
-        t, d = n // GROUP, n % GROUP
-        to_lat = (lat + n_lat - away(t) % n_lat) % n_lat
-        to_quad = (lon // GROUP + quads - t % quads) % quads
-        target = to_lat * n_lon + to_quad * GROUP + (lon + d) % GROUP
-        pltpu.make_async_remote_copy(
-            src_ref=send.at[rows_of(target), :],
-            dst_ref=recv.at[rows_of(me), :],
-            send_sem=out_sem,
-            recv_sem=in_sem.at[my_group],
-            device_id=on_tile(target),
-            device_id_type=MESH,
-        ).start()
+    my_group = lat * quads + quad
+
+    def deliver(t, carry):
+        to_lat = lax.rem(lat + n_lat - away(t), n_lat)
+        to_quad = lax.rem(quad + quads - lax.rem(t, quads), quads)
+        for d in range(GROUP):
+            to_lon = to_quad * GROUP + lax.rem(place + d, GROUP)
+            transfer = pltpu.make_async_remote_copy(
+                src_ref=send.at[rows_of(to_lat * n_lon + to_lon), :],
+                dst_ref=recv.at[rows_of(me), :],
+                send_sem=out_sem,
+                recv_sem=in_sem.at[my_group],
+                device_id={"lat": to_lat, "lon": to_lon},
+                device_id_type=MESH,
+            )
+            if d:
+                transfer.start()
+            else:
+                pl.when(t > 0)(transfer.start)
         return carry
 
     pltpu.make_async_copy(send.at[rows_of(me), :], recv.at[rows_of(me), :], in_sem.at[my_group]).start()
-    lax.fori_loop(1, tiles, deliver, 0)
+    lax.fori_loop(0, groups, deliver, 0)
     total[...] = jnp.zeros_like(total)
+    index[...] = iota(index.shape, 0).astype(F32).astype(BF16)
     height = GROUP * ROWS
 
     def group_of(t):
-        from_lat = (lat + away(t)) % n_lat
-        from_quad = (lon // GROUP + t % quads) % quads
-        return from_lat * quads + from_quad
+        from_lat = lax.rem(lat + away(t), n_lat)
+        return from_lat * quads + lax.rem(quad + lax.rem(t, quads), quads)
 
     def await_group(t):
         g = group_of(t)
@@ -331,7 +342,7 @@
         pltpu.make_async_copy(landed, landed, in_sem.at[g]).wait()
 
     def weigh_next(t, lhs, rhs):
-        weigh_group(recv, group_of(t) * height, 2 * rows, cols, lhs, rhs)
+        weigh_group(recv, group_of(t) * height, 2 * rows, cols, index, lhs, rhs)
 
     await_group(0)
     weigh_next(0, lhs_a, rhs_a)
@@ -340,17 +351,16 @@
         await_group(2 * i + 1)
         weigh_next(2 * i + 1, lhs_b, rhs_b)
         add_group(lhs_a, rhs_a, total)
-        following = jnp.minimum(2 * i + 2, groups - 1)
-
-        @pl.when(i < groups // 2 - 1)
-        def _():
-            await_group(following)
-
-        weigh_next(following, lhs_a, rhs_a)
+        await_group(2 * i + 2)
+        weigh_next(2 * i + 2, lhs_a, rhs_a)
         add_group(lhs_b, rhs_b, total)
         return carry
 
-    lax.fori_loop(0, groups // 2, spread_two, 0)
+    lax.fori_loop(0, groups // 2 - 1, spread_two, 0)
+    await_group(groups - 1)
+    weigh_next(groups - 1, lhs_b, rhs_b)
+    add_group(lhs_a, rhs_a, total)
+    add_group(lhs_b, rhs_b, total)
     gone = send.at[pl.ds(0, (tiles - 1) * ROWS), :]
     pltpu.make_async_copy(gone, gone, out_sem).wait()
     unpack(total, 2 * rows, cols, part)
@@ -437,22 +447,15 @@
                 device_id_type=MESH,
             )
 
-        def begin(d, carry):
-            copy_of(me, d, (me + d) % count).start()
-            return carry
-
-        def arrive(d, carry):
-            copy_of((me + count - d) % count, d, (me + d) % count).wait_recv()
-            return carry
-
-        def leave(d, carry):
-            copy_of(me, d, (me + d) % count).wait_send()
-            return carry
-
-        lax.fori_loop(1, count, begin, 0)
+        half = count // 2
+        offsets = [half] + [half + s * k for k in range(1, half) for s in (1, -1)]
+        for d in offsets:
+            copy_of(me, d, lax.rem(me + d, count)).start()
         at[me] = value[...]
-        lax.fori_loop(1, count, arrive, 0)
-        lax.fori_loop(1, count, leave, 0)
+        for d in reversed(offsets):
+            copy_of(lax.rem(me + count - d, count), d, lax.rem(me + d, count)).wait_recv()
+        for d in offsets:
+            copy_of(me, d, lax.rem(me + d, count)).wait_send()
         return add_up([at[k] for k in range(count)])
 
     rank_in[...] = share(n_lon, lon, on_line, line_in, line_at, line_send, line_recv)
@@ -482,7 +485,7 @@
     tiles = n_lat * n_lon
     groups = tiles // GROUP
     tall = total_shape(2 * rows, cols)
-    deep = GROUP * CAP * LANE
+    deep = GROUP * CAP
     return pl.pallas_call(
         functools.partial(step_kernel, n_lat, n_lon),
         out_shape=(own, own, own, jax.ShapeDtypeStruct((1, LANE), F32)),
@@ -491,10 +494,11 @@
         scratch_shapes=[
             pltpu.VMEM((tiles * ROWS, LANE), F32),
             pltpu.VMEM((tiles * ROWS, LANE), F32),
-            pltpu.VMEM((tall[0], deep), BF16),
-            pltpu.VMEM((tall[1], deep), BF16),
-            pltpu.VMEM((tall[0], deep), BF16),
-            pltpu.VMEM((tall[1], deep), BF16),
+            pltpu.VMEM((deep, tall[0], LANE), BF16),
+            pltpu.VMEM((deep, tall[1], LANE), BF16),
+            pltpu.VMEM((deep, tall[0], LANE), BF16),
+            pltpu.VMEM((deep, tall[1], LANE), BF16),
+            pltpu.VMEM((tall[1], LANE), BF16),
             pltpu.VMEM(tall, F32),
             pltpu.VMEM((2, rows + EDGE, cols + LANE), F32),
             pltpu.VMEM((rows + EDGE, cols + LANE), F32),
@@ -538,20 +542,23 @@
     return block
 
 
-def stepwise(forcing, land, inertia, depth):
-    conduct = land.astype(F32) * depth
-    padded = border(conduct)
-    north = jnp.sqrt(conduct * padded[:-2, 1:-1])
-    south = jnp.sqrt(conduct * padded[2:, 1:-1])
-    west = jnp.sqrt(conduct * padded[1:-1, :-2])
-    east = jnp.sqrt(conduct * padded[1:-1, 2:])
-    diagonal = inertia + north + south + west + east
-
+def stepwise(sound, field, residual, forcing, land, own, sea):
     def whole(value):
         return lax.psum(jnp.sum(value), ("lat", "lon", "obs"))
 
     def step(_, state):
-        field, residual, direction, norm = state
+        (field, residual, direction, before), depth, inertia = lax.optimization_barrier(
+            (state, sea, own)
+        )
+        conduct = land.astype(F32) * depth
+        padded = border(conduct)
+        north = jnp.sqrt(conduct * padded[:-2, 1:-1])
+        south = jnp.sqrt(conduct * padded[2:, 1:-1])
+        west = jnp.sqrt(conduct * padded[1:-1, :-2])
+        east = jnp.sqrt(conduct * padded[1:-1, 2:])
+        diagonal = inertia + north + south + west + east
+        norm = whole(residual * residual)
+        direction = residual + norm / before * direction
         outer = border(direction)
         applied = (
             diagonal * direction
@@ -561,23 +568,21 @@
             - east * outer[1:-1, 2:]
         )
         size = norm / whole(direction * applied)
-        field = field + size * direction
-        residual = residual - size * applied
-        after = whole(residual * residual)
-        return field, residual, residual + after / norm * direction, after
-
-    state = (jnp.zeros_like(forcing), forcing, forcing, whole(forcing * forcing))
-    return lax.fori_loop(0, ITERS, step, state)[:2]
+        return field + size * direction, residual - size * applied, direction, norm
+
+    state = (
+        jnp.where(sound, field, 0.0),
+        jnp.where(sound, residual, forcing),
+        jnp.zeros_like(forcing),
+        jnp.float32(1.0),
+    )
+    return lax.fori_loop(0, jnp.where(sound, 0, ITERS), step, state)[:2]
 
 
 def body(n_lat, n_lon, *inputs):
     land, inertia, depth = inputs[-3:]
     field, residual, forcing, sound = step(n_lat, n_lon, *inputs)
-    return lax.cond(
-        sound[0, 0] > 0.5,
-        lambda: (field, residual),
-        lambda: stepwise(forcing, land, inertia, depth),
-    )
+    return stepwise(sound[0, 0] > 0.5, field, residual, forcing, land, inertia, depth)
 
 
 def solution(mesh):

time: 95.2 us -> 89 us (0.935)
  Pallas kernels: 90.5 us -> 84 us
  other arithmetic: 0 us -> 1.96 us
  local copies, waits for them, and re-layouts: 2.9 us -> 1.33 us
    pallas_call x1, Pallas kernels: 90.5 us -> 84 us  [step(): pl.pallas_call(functools.partial(step_kernel, n_lat, n_lon), out_shape=(o...]
    unnamed x10, local copies, waits for them, and re-layouts: 2.89 us -> 1.32 us
    select_n x0 -> x1, other arithmetic: none -> 1 us  [stepwise(): jnp.where(sound, field, 0.0)]
    convert_element_type x0 -> x1, other arithmetic: none -> 0.96 us  [step(): conduct = land.astype(F32) * depth]
where the time goes in v3:
time: 89 us; the launch traced here: 88.9 us
  Pallas kernels  84 us (94%)
  other arithmetic  1.96 us (2%)
  between operations  1.4 us (2%)
  local copies, waits for them, and re-layouts  1.33 us (1%)
    pallas_call x1, Pallas kernels, step(): pl.pallas_call(functools.partial(step_kernel, n_lat, n_lon), out_shape=(o...  84 us

profile of v3, /device:TPU:1, one launch (start us, length us, event | category | flops | bytes accessed | tf_op | source)
XLA Modules:
  0.0 88.9 jit_solution(7441365105306237497)
XLA Ops:
  1.3 0.0 copy-start.1
  1.3 0.0 copy-start.2
  1.3 1.0 %convert_element_type.5 = f32[32,1024]{1,0:T(8,128)S(1)} convert(s32[32,1024]{1,0:T(8,128)} %land.1) | non-fusion elementwise | flops 32768 | bytes 262144 | tf_op jit(solution)/shard_map/while/body/convert_element_type | solution.py:553
  2.3 0.0 copy-done.1
  2.3 0.0 copy-done.2
  2.3 84.0 %shard_map.104 = (f32[32,1024]{1,0:T(8,128)}, f32[32,1024]{1,0:T(8,128)}, f32[32,1024]{1,0:T(8,128)}, f32[1,128]{1,0:T(1,128)}) custom-call(f32[128,128]{1,0:T(8,128)} %innovation.1, f32[128,128]{1,0:T(8,128)} %error.1, f32[2,128,128]{2,1,0:T(8,128)} %offset.1, s32[128,128]{1,0:T(8,128)} %cell.1, s32[1,128]{1,0:T(1,128)} %owner.1, s32[1]{0:T(128)S(6)} %copy.28.count, ...), custom_call_target="tpu_custom_call" | custom-call | tf_op jit(solution)/shard_map/pallas_call | solution.py:489
  86.3 0.0 copy-start.4
  86.3 0.6 copy-done.4
  87.0 1.0 %broadcast_select_fusion = (f32[32,1024]{1,0:T(8,128)S(1)}, f32[32,1024]{1,0:T(8,128)S(1)}) fusion(f32[32,1024]{1,0:T(8,128)} %get-tuple-element.122, pred[]{:T(512)} %bitcast, f32[32,1024]{1,0:T(8,128)} %get-tuple-element.123, f32[32,1024]{1,0:T(8,128)} %get-tuple-element.124), kind=kLoop, calls=%fused_computation.43 | loop fusion | flops 65536 | bytes 655361 | tf_op jit(solution)/shard_map/jit(_where)/select_n | solution.py:574
  88.0 0.2 while.18
  88.2 0.0 copy-start
  88.2 0.0 copy-start.3
  88.2 0.6 copy-done
  88.8 0.0 copy-done.3
  (1 shorter events, 0.0 us)
Async XLA Ops:
  1.3 1.0 %copy-start.1 = (f32[32,1024]{1,0:T(8,128)S(1)}, f32[32,1024]{1,0:T(8,128)}, u32[]{:S(2)}) copy-start(f32[32,1024]{1,0:T(8,128)} %depth.1) | copy-start | bytes 393220
  1.3 1.0 %copy-start.2 = (f32[32,1024]{1,0:T(8,128)S(1)}, f32[32,1024]{1,0:T(8,128)}, u32[]{:S(2)}) copy-start(f32[32,1024]{1,0:T(8,128)} %inertia.1) | copy-start | bytes 393220
  86.3 0.6 copy-start.4
  88.2 0.7 copy-start
  88.2 0.7 copy-start.3

commit v4 on v3

--- a/solution.py
+++ b/solution.py
@@ -22,6 +22,7 @@
 CENTRE = 9.0
 RADIUS = 9.0
 TRUST = 1000.0
+AHEAD = 6
 
 
 def iota(shape, dim):
@@ -327,7 +328,7 @@
         return carry
 
     pltpu.make_async_copy(send.at[rows_of(me), :], recv.at[rows_of(me), :], in_sem.at[my_group]).start()
-    lax.fori_loop(0, groups, deliver, 0)
+    lax.fori_loop(0, min(AHEAD, groups), deliver, 0)
     total[...] = jnp.zeros_like(total)
     index[...] = iota(index.shape, 0).astype(F32).astype(BF16)
     height = GROUP * ROWS
@@ -348,6 +349,8 @@
     weigh_next(0, lhs_a, rhs_a)
 
     def spread_two(i, carry):
+        begin = jnp.minimum(2 * i + AHEAD, groups)
+        lax.fori_loop(begin, jnp.minimum(begin + 2, groups), deliver, 0)
         await_group(2 * i + 1)
         weigh_next(2 * i + 1, lhs_b, rhs_b)
         add_group(lhs_a, rhs_a, total)

time: 89 us -> 88.7 us (level)
  no operation moved by 1% of the time
where the time goes in v4:
time: 88.7 us; the launch traced here: 88.5 us
  Pallas kernels  83.6 us (94%)
  other arithmetic  1.96 us (2%)
  between operations  1.4 us (2%)
  local copies, waits for them, and re-layouts  1.33 us (1%)
    pallas_call x1, Pallas kernels, step(): pl.pallas_call(functools.partial(step_kernel, n_lat, n_lon), out_shape=(o...  83.6 us

profile of v4, /device:TPU:1, one launch (start us, length us, event | category | flops | bytes accessed | tf_op | source)
XLA Modules:
  0.0 88.5 jit_solution(16688288882452370255)
XLA Ops:
  1.3 0.0 copy-start.1
  1.3 0.0 copy-start.2
  1.3 1.0 %convert_element_type.5 = f32[32,1024]{1,0:T(8,128)S(1)} convert(s32[32,1024]{1,0:T(8,128)} %land.1) | non-fusion elementwise | flops 32768 | bytes 262144 | tf_op jit(solution)/shard_map/while/body/convert_element_type | solution.py:556
  2.3 0.0 copy-done.1
  2.3 0.0 copy-done.2
  2.3 83.6 %shard_map.104 = (f32[32,1024]{1,0:T(8,128)}, f32[32,1024]{1,0:T(8,128)}, f32[32,1024]{1,0:T(8,128)}, f32[1,128]{1,0:T(1,128)}) custom-call(f32[128,128]{1,0:T(8,128)} %innovation.1, f32[128,128]{1,0:T(8,128)} %error.1, f32[2,128,128]{2,1,0:T(8,128)} %offset.1, s32[128,128]{1,0:T(8,128)} %cell.1, s32[1,128]{1,0:T(1,128)} %owner.1, s32[1]{0:T(128)S(6)} %copy.28.count, ...), custom_call_target="tpu_custom_call" | custom-call | tf_op jit(solution)/shard_map/pallas_call | solution.py:492
  86.0 0.0 copy-start.4
  86.0 0.6 copy-done.4
  86.6 1.0 %broadcast_select_fusion = (f32[32,1024]{1,0:T(8,128)S(1)}, f32[32,1024]{1,0:T(8,128)S(1)}) fusion(f32[32,1024]{1,0:T(8,128)} %get-tuple-element.122, pred[]{:T(512)} %bitcast, f32[32,1024]{1,0:T(8,128)} %get-tuple-element.123, f32[32,1024]{1,0:T(8,128)} %get-tuple-element.124), kind=kLoop, calls=%fused_computation.43 | loop fusion | flops 65536 | bytes 655361 | tf_op jit(solution)/shard_map/jit(_where)/select_n | solution.py:577
  87.6 0.2 while.18
  87.8 0.0 copy-start
  87.8 0.0 copy-start.3
  87.8 0.6 copy-done
  88.5 0.0 copy-done.3
  (1 shorter events, 0.0 us)
Async XLA Ops:
  1.3 1.0 %copy-start.1 = (f32[32,1024]{1,0:T(8,128)S(1)}, f32[32,1024]{1,0:T(8,128)}, u32[]{:S(2)}) copy-start(f32[32,1024]{1,0:T(8,128)} %depth.1) | copy-start | bytes 393220
  1.3 1.0 %copy-start.2 = (f32[32,1024]{1,0:T(8,128)S(1)}, f32[32,1024]{1,0:T(8,128)}, u32[]{:S(2)}) copy-start(f32[32,1024]{1,0:T(8,128)} %inertia.1) | copy-start | bytes 393220
  86.0 0.6 copy-start.4
  87.8 0.7 copy-start
  87.8 0.7 copy-start.3

commit v5 on v4

--- a/solution.py
+++ b/solution.py
@@ -11,7 +11,7 @@
 CAP = 3
 FIELDS = 4
 ROWS = CAP * FIELDS
-GROUP = 8
+GROUP = 4
 SPLIT = 4
 PART = SPLIT + 1
 LANE = 128
@@ -22,7 +22,7 @@
 CENTRE = 9.0
 RADIUS = 9.0
 TRUST = 1000.0
-AHEAD = 6
+AHEAD = 12
 
 
 def iota(shape, dim):

time: 88.7 us -> 92.5 us (1.043)
  Pallas kernels: 83.6 us -> 87.5 us
    pallas_call x1, Pallas kernels: 83.6 us -> 87.5 us  [step(): pl.pallas_call(functools.partial(step_kernel, n_lat, n_lon), out_shape=(o...]
where the time goes in v5:
time: 92.5 us; the launch traced here: 92.4 us
  Pallas kernels  87.5 us (95%)
  other arithmetic  1.96 us (2%)
  between operations  1.4 us (2%)
  local copies, waits for them, and re-layouts  1.33 us (1%)
    pallas_call x1, Pallas kernels, step(): pl.pallas_call(functools.partial(step_kernel, n_lat, n_lon), out_shape=(o...  87.5 us

profile of v5, /device:TPU:1, one launch (start us, length us, event | category | flops | bytes accessed | tf_op | source)
XLA Modules:
  0.0 92.4 jit_solution(16294492952987684151)
XLA Ops:
  1.3 0.0 copy-start.1
  1.3 0.0 copy-start.2
  1.3 1.0 %convert_element_type.5 = f32[32,1024]{1,0:T(8,128)S(1)} convert(s32[32,1024]{1,0:T(8,128)} %land.1) | non-fusion elementwise | flops 32768 | bytes 262144 | tf_op jit(solution)/shard_map/while/body/convert_element_type | solution.py:556
  2.3 0.0 copy-done.1
  2.3 0.0 copy-done.2
  2.3 87.5 %shard_map.104 = (f32[32,1024]{1,0:T(8,128)}, f32[32,1024]{1,0:T(8,128)}, f32[32,1024]{1,0:T(8,128)}, f32[1,128]{1,0:T(1,128)}) custom-call(f32[128,128]{1,0:T(8,128)} %innovation.1, f32[128,128]{1,0:T(8,128)} %error.1, f32[2,128,128]{2,1,0:T(8,128)} %offset.1, s32[128,128]{1,0:T(8,128)} %cell.1, s32[1,128]{1,0:T(1,128)} %owner.1, s32[1]{0:T(128)S(6)} %copy.28.count, ...), custom_call_target="tpu_custom_call" | custom-call | tf_op jit(solution)/shard_map/pallas_call | solution.py:492
  89.8 0.0 copy-start.4
  89.8 0.6 copy-done.4
  90.4 1.0 %broadcast_select_fusion = (f32[32,1024]{1,0:T(8,128)S(1)}, f32[32,1024]{1,0:T(8,128)S(1)}) fusion(f32[32,1024]{1,0:T(8,128)} %get-tuple-element.122, pred[]{:T(512)} %bitcast, f32[32,1024]{1,0:T(8,128)} %get-tuple-element.123, f32[32,1024]{1,0:T(8,128)} %get-tuple-element.124), kind=kLoop, calls=%fused_computation.43 | loop fusion | flops 65536 | bytes 655361 | tf_op jit(solution)/shard_map/jit(_where)/select_n | solution.py:577
  91.5 0.2 while.18
  91.7 0.0 copy-start
  91.7 0.0 copy-start.3
  91.7 0.6 copy-done
  92.3 0.0 copy-done.3
  (1 shorter events, 0.0 us)
Async XLA Ops:
  1.3 1.0 %copy-start.1 = (f32[32,1024]{1,0:T(8,128)S(1)}, f32[32,1024]{1,0:T(8,128)}, u32[]{:S(2)}) copy-start(f32[32,1024]{1,0:T(8,128)} %depth.1) | copy-start | bytes 393220
  1.3 1.0 %copy-start.2 = (f32[32,1024]{1,0:T(8,128)S(1)}, f32[32,1024]{1,0:T(8,128)}, u32[]{:S(2)}) copy-start(f32[32,1024]{1,0:T(8,128)} %inertia.1) | copy-start | bytes 393220
  89.8 0.6 copy-start.4
  91.7 0.7 copy-start
  91.7 0.7 copy-start.3

commit v6 on v4

--- a/solution.py
+++ b/solution.py
@@ -352,11 +352,11 @@
         begin = jnp.minimum(2 * i + AHEAD, groups)
         lax.fori_loop(begin, jnp.minimum(begin + 2, groups), deliver, 0)
         await_group(2 * i + 1)
+        add_group(lhs_a, rhs_a, total)
         weigh_next(2 * i + 1, lhs_b, rhs_b)
-        add_group(lhs_a, rhs_a, total)
         await_group(2 * i + 2)
+        add_group(lhs_b, rhs_b, total)
         weigh_next(2 * i + 2, lhs_a, rhs_a)
-        add_group(lhs_b, rhs_b, total)
         return carry
 
     lax.fori_loop(0, groups // 2 - 1, spread_two, 0)

time: 88.7 us -> 88.7 us (level)
  no operation moved by 1% of the time
where the time goes in v6:
time: 88.7 us; the launch traced here: 88.5 us
  Pallas kernels  83.6 us (94%)
  other arithmetic  1.96 us (2%)
  between operations  1.4 us (2%)
  local copies, waits for them, and re-layouts  1.33 us (1%)
    pallas_call x1, Pallas kernels, step(): pl.pallas_call(functools.partial(step_kernel, n_lat, n_lon), out_shape=(o...  83.6 us

profile of v6, /device:TPU:1, one launch (start us, length us, event | category | flops | bytes accessed | tf_op | source)
XLA Modules:
  0.0 88.5 jit_solution(16688288882452370255)
XLA Ops:
  1.3 0.0 copy-start.1
  1.3 0.0 copy-start.2
  1.3 1.0 %convert_element_type.5 = f32[32,1024]{1,0:T(8,128)S(1)} convert(s32[32,1024]{1,0:T(8,128)} %land.1) | non-fusion elementwise | flops 32768 | bytes 262144 | tf_op jit(solution)/shard_map/while/body/convert_element_type | solution.py:556
  2.3 0.0 copy-done.1
  2.3 0.0 copy-done.2
  2.3 83.6 %shard_map.104 = (f32[32,1024]{1,0:T(8,128)}, f32[32,1024]{1,0:T(8,128)}, f32[32,1024]{1,0:T(8,128)}, f32[1,128]{1,0:T(1,128)}) custom-call(f32[128,128]{1,0:T(8,128)} %innovation.1, f32[128,128]{1,0:T(8,128)} %error.1, f32[2,128,128]{2,1,0:T(8,128)} %offset.1, s32[128,128]{1,0:T(8,128)} %cell.1, s32[1,128]{1,0:T(1,128)} %owner.1, s32[1]{0:T(128)S(6)} %copy.28.count, ...), custom_call_target="tpu_custom_call" | custom-call | tf_op jit(solution)/shard_map/pallas_call | solution.py:492
  86.0 0.0 copy-start.4
  86.0 0.6 copy-done.4
  86.6 1.0 %broadcast_select_fusion = (f32[32,1024]{1,0:T(8,128)S(1)}, f32[32,1024]{1,0:T(8,128)S(1)}) fusion(f32[32,1024]{1,0:T(8,128)} %get-tuple-element.122, pred[]{:T(512)} %bitcast, f32[32,1024]{1,0:T(8,128)} %get-tuple-element.123, f32[32,1024]{1,0:T(8,128)} %get-tuple-element.124), kind=kLoop, calls=%fused_computation.43 | loop fusion | flops 65536 | bytes 655361 | tf_op jit(solution)/shard_map/jit(_where)/select_n | solution.py:577
  87.6 0.2 while.18
  87.8 0.0 copy-start
  87.8 0.0 copy-start.3
  87.8 0.6 copy-done
  88.5 0.0 copy-done.3
  (1 shorter events, 0.0 us)
Async XLA Ops:
  1.3 1.0 %copy-start.1 = (f32[32,1024]{1,0:T(8,128)S(1)}, f32[32,1024]{1,0:T(8,128)}, u32[]{:S(2)}) copy-start(f32[32,1024]{1,0:T(8,128)} %depth.1) | copy-start | bytes 393220
  1.3 1.0 %copy-start.2 = (f32[32,1024]{1,0:T(8,128)S(1)}, f32[32,1024]{1,0:T(8,128)}, u32[]{:S(2)}) copy-start(f32[32,1024]{1,0:T(8,128)} %inertia.1) | copy-start | bytes 393220
  86.0 0.6 copy-start.4
  87.8 0.7 copy-start
  87.8 0.7 copy-start.3
